TPU v7x, 32 devices: a whole 2x2x4 slice. The times are simulated.
32 devices in a mesh: rows: 32 (over z, y, x, core).
Axes of the slice: x: 2, y: 2, z: 4, core: 2. Of those that a mesh axis runs over, the one named last changes fastest.
Arguments:
- right_side: float32 [9, 4096], P(None, 'rows'), may hold values from -30 to 30
- diag_blocks: float32 [9, 9, 4096], P(None, None, 'rows'), may hold values from -40 to 45, as said below
- precond: float32 [9, 9, 4096], P(None, None, 'rows'), may hold values from -5 to 5, as said below
- upper_blocks: float32 [8, 9, 9, 4096], P(None, None, None, 'rows'), may hold values from -0.21875 to 0.21875
- block_cols: int32 [8, 4096], P(None, 'rows'), may hold values from 0 to 4095, as said below
- slot_of_camera: int32 [4096], replicated, may hold values from 0 to 4095, as said below
Outputs:
- solution: float32 [9, 4096], P(None, 'rows')
- residual: float32 [9, 4096], P(None, 'rows')
Inputs may be any that keep to these rules, and one draw needn't show every extreme that they name: slot_of_camera is a permutation; slot s is held by the device s // 128. `block_cols`: for every device d and every device e, exactly 32 of the entries of the lists of the rows held by d name cameras whose slot is held by e. A list may name a camera more than once, or the row's own camera; every entry adds its block. `diag_blocks`: each 9 x 9 block over the first two dimensions is symmetric positive definite. `precond`: each 9 x 9 block over the first two dimensions is symmetric positive definite.
All inputs are finite; a program needn't handle non-finite values.
Results may differ from a plain program's by a relative error of at most 0.0001.
Values sent between devices are 32-bit elements; how exact they have to be, the bound alone decides.
No kernel may reach another device: no remote copies, remote signals or barrier semaphores. Data moves between devices by JAX's collectives and lax.ppermute only.
A program may use at most 64 MiB of HBM per device.

v0:
```python
import jax
import jax.numpy as jnp
from jax import lax
from jax.sharding import PartitionSpec as P

BLOCK = 9
ITERS = 2


def residual_dot(residual, precond_res):
    return lax.psum(jnp.sum(residual * precond_res), "rows")


def local(right_side, diag_blocks, precond, upper_blocks, block_cols, slot_of_camera):
    highest = lax.Precision.HIGHEST
    cam_rows = right_side.shape[1]
    list_len = block_cols.shape[0]
    devices = lax.axis_size("rows")
    slot_lists = slot_of_camera[block_cols]
    flat_slots = slot_lists.reshape(-1)
    owners = flat_slots // cam_rows
    offsets = flat_slots % cam_rows
    bucket_order = jnp.argsort(owners, stable=True)
    inverse_order = jnp.argsort(bucket_order)
    wanted = offsets[bucket_order].reshape(devices, -1)
    requested = lax.all_to_all(wanted, "rows", split_axis=0, concat_axis=0, tiled=True)
    requested_flat = requested.reshape(-1)

    def apply_precond(operand):
        return jnp.einsum("abc,bc->ac", precond, operand, precision=highest)

    solution = jnp.zeros_like(right_side)
    residual = right_side
    precond_res = apply_precond(residual)
    direction = precond_res
    res_dot = residual_dot(residual, precond_res)
    for step in range(ITERS):
        result = jnp.einsum("abc,bc->ac", diag_blocks, direction, precision=highest)
        spread = jnp.einsum("kabc,ac->bkc", upper_blocks, direction, precision=highest).reshape(
            BLOCK, -1
        )
        answers = direction[:, requested_flat].reshape(BLOCK, devices, -1)
        outgoing = spread[:, bucket_order].reshape(BLOCK, devices, -1)
        fetched = lax.all_to_all(answers, "rows", split_axis=1, concat_axis=1, tiled=True)
        pushed = lax.all_to_all(outgoing, "rows", split_axis=1, concat_axis=1, tiled=True)
        gathered = fetched.reshape(BLOCK, -1)[:, inverse_order].reshape(BLOCK, list_len, cam_rows)
        result = result + jnp.einsum("kabc,bkc->ac", upper_blocks, gathered, precision=highest)
        result = result.at[:, requested_flat].add(pushed.reshape(BLOCK, -1))
        step_size = res_dot / lax.psum(jnp.sum(direction * result), "rows")
        solution = solution + step_size * direction
        residual = residual - step_size * result
        if step + 1 < ITERS:
            precond_res = apply_precond(residual)
            new_dot = residual_dot(residual, precond_res)
            direction = precond_res + new_dot / res_dot * direction
            res_dot = new_dot
    return (solution, residual)


def solution(mesh):
    return jax.shard_map(
        local,
        mesh=mesh,
        in_specs=(
            P(None, "rows"),
            P(None, None, "rows"),
            P(None, None, "rows"),
            P(None, None, None, "rows"),
            P(None, "rows"),
            P(),
        ),
        out_specs=(P(None, "rows"), P(None, "rows")),
        check_vma=False,
    )
```

profile of v0, /device:TPU:0, one launch (start us, length us, event | category | flops | bytes accessed | tf_op | source)
XLA Modules:
  0.0 278.7 jit_solution(16543948351234514797)
XLA Ops:
  0.7 0.7 fusion.5
  1.4 6.1 %gather_fusion = s32[1024]{0:T(1024)S(1)} fusion(s32[4096]{0:T(1024)S(1)} %copy-done, s32[1024]{0:T(1024)S(1)} %fusion.5), kind=kCustom, calls=%fused_computation | custom fusion | bytes 12288 | tf_op jit(solution)/shard_map/gather | solution.py:19
  7.6 4.4 %sort.34 = (s32[1024]{0:T(1024)}, s32[1024]{0:T(1024)S(1)}) sort(s32[1024]{0:T(1024)S(1)} %get-tuple-element.16, s32[1024]{0:T(1024)S(1)} %iota.8), dimensions={0}, to_apply=%region_2.3 | sort | flops 10240 | bytes 16384 | tf_op jit(solution)/shard_map/jit(argsort)/sort | solution.py:23
  12.0 4.5 %gather_fusion.1 = s32[1024]{0:T(1024)S(1)} fusion(s32[1024]{0:T(1024)S(1)} %get-tuple-element.17, s32[1024]{0:T(1024)S(1)} %fusion.6), kind=kCustom, calls=%fused_computation.1 | custom fusion | bytes 12288 | tf_op jit(solution)/shard_map/gather | solution.py:25
  16.5 0.7 all_to_all.18
  17.2 7.3 %all-to-all-start = ((s32[32,1,32]{2,1,0:T(1,128)}), s32[32,1,32]{2,1,0:T(1,128)S(1)}, u32[]{:S(2)}, u32[]{:S(2)}) async-start(s32[32,1,32]{2,1,0:T(1,128)} %all_to_all.18), calls=%async_computation | async-start | bytes 32768 | tf_op jit(solution)/shard_map/all_to_all | solution.py:26
  25.2 8.2 %copy.42 = f32[8,9,9,128]{2,1,0,3:T(8,128)} copy(f32[8,9,9,128]{3,0,2,1:T(8,128)S(1)} %copy-done.1) | data formatting | bytes 663552 | tf_op args[3]
  33.4 6.5 %fusion.11 = f32[128,1,8,9]{3,1,2,0:T(1,128)S(1)} fusion(f32[9,128,1,1]{0,2,3,1:T(1,128)S(1)} %bitcast.108, f32[8,9,9,128]{2,1,0,3:T(8,128)} %copy.42), kind=kOutput, calls=%fused_computation.43 | convolution fusion | flops 995328 | bytes 373248 | tf_op jit(solution)/shard_map/kabc,ac->bkc/dot_general | solution.py:39
  40.0 1.0 fusion.10
  41.0 4.4 %sort.35 = (s32[1024]{0:T(1024)}, s32[1024]{0:T(1024)S(1)}) sort(s32[1024]{0:T(1024)S(1)} %get-tuple-element.4, s32[1024]{0:T(1024)S(1)} %iota.9), dimensions={0}, to_apply=%region_3.4 | sort | flops 10240 | bytes 16384 | tf_op jit(solution)/shard_map/jit(argsort)/sort | solution.py:24
  45.4 2.8 %gather_fusion.4 = f32[1024,9]{1,0:T(8,128)S(1)} fusion(f32[9,1024]{0,1:T(8,128)S(1)} %bitcast.116, s32[1024]{0:T(1024)S(1)} %fusion.6), kind=kCustom, calls=%fused_computation.4 | custom fusion | bytes 77824 | tf_op jit(solution)/shard_map/gather | solution.py:43
  48.5 0.8 reshape.208
  49.3 5.8 %all-to-all-start.2 = ((f32[32,1,288]{2,1,0:T(1,128)}), f32[32,1,288]{2,1,0:T(1,128)S(1)}, u32[]{:S(2)}, u32[]{:S(2)}) async-start(f32[32,1,288]{2,1,0:T(1,128)} %reshape.208), calls=%async_computation.2 | async-start | bytes 98304 | tf_op jit(solution)/shard_map/all_to_all | solution.py:45
  55.6 0.7 reduce.5
  56.4 2.8 %gather_fusion.2 = f32[1024,9]{1,0:T(8,128)S(1)} fusion(f32[9,128]{0,1:T(8,128)S(1)} %bitcast.110, s32[1024]{0:T(1024)S(1)} %broadcast_clamp_fusion), kind=kCustom, calls=%fused_computation.2 | custom fusion | bytes 77824 | tf_op jit(solution)/shard_map/gather | solution.py:42
  59.5 0.8 reshape.206
  60.3 2.2 all-to-all-done.2
  62.5 3.8 %all-to-all-start.1 = ((f32[32,1,288]{2,1,0:T(1,128)}), f32[32,1,288]{2,1,0:T(1,128)S(1)}, u32[]{:S(2)}, u32[]{:S(2)}) async-start(f32[32,1,288]{2,1,0:T(1,128)} %reshape.206), calls=%async_computation.1 | async-start | bytes 98304 | tf_op jit(solution)/shard_map/all_to_all | solution.py:44
  66.3 8.1 %copy.39 = f32[8,9,9,128]{1,2,0,3:T(8,128)} copy(f32[8,9,9,128]{3,0,2,1:T(8,128)S(1)} %copy-done.1) | data formatting | bytes 663552 | tf_op args[3]
  75.6 0.8 reduce.7
  76.4 1.1 copy.20
  77.5 0.8 reduce.6
  78.6 2.8 %gather_fusion.3 = f32[1024,9]{1,0:T(8,128)S(1)} fusion(f32[9,1024]{0,1:T(8,128)S(1)} %bitcast.114, s32[1024]{0:T(1024)S(1)} %fusion.7), kind=kCustom, calls=%fused_computation.3 | custom fusion | bytes 77824 | tf_op jit(solution)/shard_map/gather | solution.py:46
  81.5 9.7 %fusion.2 = f32[128,1,9,1]{2,1,3,0:T(1,128)S(1)} fusion(f32[8,9,9,128]{1,2,0,3:T(8,128)} %copy.39, f32[9,8,128,1]{0,2,1,3:T(8,128)S(1)} %bitcast.127), kind=kOutput, calls=%fused_computation.12 | convolution fusion | flops 995328 | bytes 373248 | tf_op jit(solution)/shard_map/kabc,bkc->ac/dot_general | solution.py:47
  91.2 6.5 %scatter_fusion = f32[9,128]{0,1:T(8,128)S(1)} fusion(f32[9,128]{0,1:T(8,128)S(1)} %add_bitcast_fusion.1, s32[1024]{0:T(1024)S(1)} %bitcast.141, f32[1024,9]{1,0:T(8,128)} %bitcast.129), kind=kCustom, calls=%fused_computation.8 | custom fusion | flops 9216 | bytes 114688 | tf_op jit(solution)/shard_map/scatter-add | solution.py:48
  97.7 0.6 multiply_reduce_fusion.3
  98.3 40.5 %all-reduce = (f32[]{:T(128)}, f32[]{:T(128)}) all-reduce(f32[]{:T(128)} %get-tuple-element.13, f32[]{:T(128)} %get-tuple-element.12), channel_id=1, replica_groups=mesh['rows'=32] {'rows'}, use_global_device_ids=true, to_apply=%region_1.2 | all-reduce | flops 2 | bytes 16 | tf_op jit(solution)/shard_map/psum | solution.py:11
  140.2 1.0 fusion.12
  141.2 0.6 multiply_reduce_fusion.2
  141.8 40.7 %psum.30 = f32[]{:T(128)} all-reduce(f32[]{:T(128)} %multiply_reduce_fusion.2), channel_id=1, replica_groups=mesh['rows'=32] {'rows'}, use_global_device_ids=true, to_apply=%region_8.9 | all-reduce | flops 1 | bytes 8 | tf_op jit(solution)/shard_map/psum | solution.py:11
  184.0 6.5 %fusion.14 = f32[128,1,8,9]{3,1,2,0:T(1,128)S(1)} fusion(f32[9,128,1,1]{0,2,3,1:T(1,128)S(1)} %bitcast.111, f32[8,9,9,128]{2,1,0,3:T(8,128)} %copy.42), kind=kOutput, calls=%fused_computation.46 | convolution fusion | flops 995328 | bytes 373248 | tf_op jit(solution)/shard_map/kabc,ac->bkc/dot_general | solution.py:39
  190.6 2.8 %gather_fusion.7 = f32[1024,9]{1,0:T(8,128)S(1)} fusion(f32[9,1024]{0,1:T(8,128)S(1)} %bitcast.115, s32[1024]{0:T(1024)S(1)} %fusion.6), kind=kCustom, calls=%fused_computation.7 | custom fusion | bytes 77824 | tf_op jit(solution)/shard_map/gather | solution.py:43
  193.7 0.8 reshape.212
  194.4 5.5 %all-to-all-start.4 = ((f32[32,1,288]{2,1,0:T(1,128)}), f32[32,1,288]{2,1,0:T(1,128)S(1)}, u32[]{:S(2)}, u32[]{:S(2)}) async-start(f32[32,1,288]{2,1,0:T(1,128)} %reshape.212), calls=%async_computation.4 | async-start | bytes 98304 | tf_op jit(solution)/shard_map/all_to_all | solution.py:45
  199.9 2.8 %gather_fusion.5 = f32[1024,9]{1,0:T(8,128)S(1)} fusion(f32[9,128]{0,1:T(8,128)S(1)} %multiply_add_fusion.1, s32[1024]{0:T(1024)S(1)} %broadcast_clamp_fusion), kind=kCustom, calls=%fused_computation.5 | custom fusion | bytes 77824 | tf_op jit(solution)/shard_map/gather | solution.py:42
  203.0 0.8 reshape.210
  203.8 3.5 %all-to-all-done.4 = f32[32,1,288]{2,1,0:T(1,128)S(1)} async-done(((f32[32,1,288]{2,1,0:T(1,128)}), f32[32,1,288]{2,1,0:T(1,128)S(1)}, u32[]{:S(2)}, u32[]{:S(2)}) %all-to-all-start.4) | async-done | bytes 36896 | tf_op jit(solution)/shard_map/all_to_all | solution.py:45
  207.3 2.6 all-to-all-start.3
  209.8 1.0 fusion.13
  210.8 0.8 reduce.9
  212.0 5.2 %all-to-all-done.3 = f32[32,1,288]{2,1,0:T(1,128)S(1)} async-done(((f32[32,1,288]{2,1,0:T(1,128)}), f32[32,1,288]{2,1,0:T(1,128)S(1)}, u32[]{:S(2)}, u32[]{:S(2)}) %all-to-all-start.3) | async-done | bytes 36896 | tf_op jit(solution)/shard_map/all_to_all | solution.py:44
  217.1 0.8 reduce.8
  218.3 2.8 %gather_fusion.6 = f32[1024,9]{1,0:T(8,128)S(1)} fusion(f32[9,1024]{0,1:T(8,128)S(1)} %bitcast.113, s32[1024]{0:T(1024)S(1)} %fusion.7), kind=kCustom, calls=%fused_computation.6 | custom fusion | bytes 77824 | tf_op jit(solution)/shard_map/gather | solution.py:46
  221.1 9.7 %fusion = f32[128,1,9,1]{2,1,3,0:T(1,128)S(1)} fusion(f32[8,9,9,128]{1,2,0,3:T(8,128)} %copy.39, f32[9,8,128,1]{0,2,1,3:T(8,128)S(1)} %bitcast.126), kind=kOutput, calls=%fused_computation.10 | convolution fusion | flops 995328 | bytes 373248 | tf_op jit(solution)/shard_map/kabc,bkc->ac/dot_general | solution.py:47
  230.8 6.1 %scatter_fusion.1 = f32[9,128]{0,1:T(8,128)S(1)} fusion(f32[9,128]{0,1:T(8,128)S(1)} %add_bitcast_fusion, s32[1024]{0:T(1024)S(1)} %bitcast.142, f32[1024,9]{1,0:T(8,128)S(1)} %bitcast.128), kind=kCustom, calls=%fused_computation.9 | custom fusion | flops 9216 | bytes 114688 | tf_op jit(solution)/shard_map/scatter-add | solution.py:48
  237.6 38.4 %psum.31 = f32[]{:T(128)} all-reduce(f32[]{:T(128)} %multiply_reduce_fusion.1), channel_id=1, replica_groups=mesh['rows'=32] {'rows'}, use_global_device_ids=true, to_apply=%region_11.12 | all-reduce | flops 1 | bytes 8 | tf_op jit(solution)/shard_map/psum | solution.py:49
  277.4 0.7 copy.26
  278.0 0.7 copy.27
  (46 shorter events, 5.6 us)
Async XLA Ops:
  0.6 0.8 copy-start
  0.6 23.9 %copy-start.4 = (f32[9,128]{1,0:T(8,128)S(1)}, f32[9,128]{1,0:T(8,128)}, u32[]{:S(2)}) copy-start(f32[9,128]{1,0:T(8,128)} %param.6) | copy-start | bytes 13828
  0.7 23.9 %copy-start.2 = (f32[9,9,128]{2,1,0:T(8,128)S(1)}, f32[9,9,128]{2,1,0:T(8,128)}, u32[]{:S(2)}) copy-start(f32[9,9,128]{2,1,0:T(8,128)} %param.8) | copy-start | bytes 124420
  0.7 24.0 %copy-start.3 = (f32[9,9,128]{2,1,0:T(8,128)S(1)}, f32[9,9,128]{2,1,0:T(8,128)}, u32[]{:S(2)}) copy-start(f32[9,9,128]{2,1,0:T(8,128)} %param.7) | copy-start | bytes 124420
  0.7 24.6 %copy-start.1 = (f32[8,9,9,128]{3,0,2,1:T(8,128)S(1)}, f32[8,9,9,128]{3,0,2,1:T(8,128)}, u32[]{:S(2)}) copy-start(f32[8,9,9,128]{3,0,2,1:T(8,128)} %param.9) | copy-start | bytes 995332
  17.2 32.1 %all-to-all-start = ((s32[32,1,32]{2,1,0:T(1,128)}), s32[32,1,32]{2,1,0:T(1,128)S(1)}, u32[]{:S(2)}, u32[]{:S(2)}) async-start(s32[32,1,32]{2,1,0:T(1,128)} %all_to_all.18), calls=%async_computation | async-start | bytes 32768 | tf_op jit(solution)/shard_map/all_to_all | solution.py:26
  49.3 13.2 %all-to-all-start.2 = ((f32[32,1,288]{2,1,0:T(1,128)}), f32[32,1,288]{2,1,0:T(1,128)S(1)}, u32[]{:S(2)}, u32[]{:S(2)}) async-start(f32[32,1,288]{2,1,0:T(1,128)} %reshape.208), calls=%async_computation.2 | async-start | bytes 98304 | tf_op jit(solution)/shard_map/all_to_all | solution.py:45
  62.5 15.1 %all-to-all-start.1 = ((f32[32,1,288]{2,1,0:T(1,128)}), f32[32,1,288]{2,1,0:T(1,128)S(1)}, u32[]{:S(2)}, u32[]{:S(2)}) async-start(f32[32,1,288]{2,1,0:T(1,128)} %reshape.206), calls=%async_computation.1 | async-start | bytes 98304 | tf_op jit(solution)/shard_map/all_to_all | solution.py:44
  194.4 12.8 %all-to-all-start.4 = ((f32[32,1,288]{2,1,0:T(1,128)}), f32[32,1,288]{2,1,0:T(1,128)S(1)}, u32[]{:S(2)}, u32[]{:S(2)}) async-start(f32[32,1,288]{2,1,0:T(1,128)} %reshape.212), calls=%async_computation.4 | async-start | bytes 98304 | tf_op jit(solution)/shard_map/all_to_all | solution.py:45
  207.3 9.9 %all-to-all-start.3 = ((f32[32,1,288]{2,1,0:T(1,128)}), f32[32,1,288]{2,1,0:T(1,128)S(1)}, u32[]{:S(2)}, u32[]{:S(2)}) async-start(f32[32,1,288]{2,1,0:T(1,128)} %reshape.210), calls=%async_computation.3 | async-start | bytes 98304 | tf_op jit(solution)/shard_map/all_to_all | solution.py:44
where the time goes:
time: 280 us; the launch traced here: 279 us
  blocking collectives  120 us (43%)
  local copies, waits for them, and re-layouts  54.8 us (20%)
  matrix products  35.5 us (13%)
  other arithmetic  27.7 us (10%)
  starting transfers between devices  25 us (9%)
  waiting for transfers between devices  10.9 us (4%)
  between operations  5.14 us (2%)
    psum x2, blocking collectives, residual_dot(): return lax.psum(jnp.sum(residual * precond_res), 'rows')  81.2 us
    psum x1, blocking collectives, local(): step_size = res_dot / lax.psum(jnp.sum(direction * result), 'rows')  38.4 us
    unnamed x25, local copies, waits for them, and re-layouts  22.3 us
    dot_general x2, matrix products, local(): jnp.einsum('kabc,bkc->ac', upper_blocks, gathered, precision=highest)  19.5 us
    dot_general x2, matrix products, local(): jnp.einsum('kabc,ac->bkc', upper_blocks, direction, precision=highest)  13 us
    scatter-add x2, other arithmetic, local(): result = result.at[:, requested_flat].add(pushed.reshape(BLOCK, -1))  12.6 us
    all_to_all x2, starting transfers between devices, local(): lax.all_to_all(outgoing, 'rows', split_axis=1, concat_axis=1, tiled=True)  11.3 us
    all_to_all x1, starting transfers between devices, local(): lax.all_to_all(wanted, 'rows', split_axis=0, concat_axis=0, tiled=True)  7.33 us
  transfers between devices with their start and end apart: 5, of which 3 were waited for; matrix products, arithmetic and copies ran while one was open for 17% of the time, Pallas kernels for 0%

commit v1 on v0

v1 whole, which is shorter than its diff:
```python
import functools
import math

import jax
import jax.numpy as jnp
from jax import lax
from jax.experimental import pallas as pl
from jax.experimental.pallas import tpu as pltpu
from jax.sharding import PartitionSpec as P

ITERS = 2
F32 = jnp.float32
BF16 = jnp.bfloat16
I32 = jnp.int32


class Sizes:
    def __init__(self, block, lists, cams, devices):
        self.block = block
        self.lists = lists
        self.cams = cams
        self.devices = devices
        self.entries = lists * cams
        self.refs = self.entries // devices
        self.groups = cams // self.refs
        self.values = block + 2
        self.push_rows = -(-self.values // self.groups)
        self.rows = block + self.push_rows
        self.shift = cams.bit_length() - 1
        assert cams == 1 << self.shift and self.refs * devices == self.entries
        assert self.refs * self.groups == cams


def split3(x):
    hi = x.astype(BF16)
    rest = x - hi.astype(F32)
    mid = rest.astype(BF16)
    low = (rest - mid.astype(F32)).astype(BF16)
    return hi, mid, low


def dot(a, b):
    return lax.dot_general(a, b, (((1,), (0,)), ((), ())), preferred_element_type=F32)


def dot_t(a, b):
    return lax.dot_general(a, b, (((1,), (1,)), ((), ())), preferred_element_type=F32)


def iota(shape, axis):
    return lax.broadcasted_iota(I32, shape, axis)


def onehot(mask):
    return jnp.where(mask, 1.0, 0.0).astype(BF16)


def col_sum(x):
    return jnp.sum(x, axis=0, keepdims=True)


def total(x):
    return jnp.sum(col_sum(x), axis=1, keepdims=True)


def block_apply(blocks_ref, v, extra=None, up_ref=None, gathered=None, sz=None):
    rows = []
    for a in range(sz.block):
        acc = blocks_ref[a] * v
        if up_ref is not None:
            for k in range(sz.lists):
                acc = acc + up_ref[k, a] * gathered[k]
        rows.append(col_sum(acc))
    out = jnp.concatenate(rows, axis=0)
    return out if extra is None else out + extra


def push(sz, v, dots, up_ref, off, pos, val_ref, perm_ref, roll_ref, msg_ref):
    c = sz.cams
    height = val_ref.shape[0]
    val_ref[...] = jnp.zeros_like(val_ref)
    for k in range(sz.lists):
        acc = up_ref[k, 0] * v[0:1]
        for a in range(1, sz.block):
            acc = acc + up_ref[k, a] * v[a : a + 1]
        lanes = slice(k * c, (k + 1) * c)
        val_ref[0 : sz.block, lanes] = acc
        val_ref[sz.block : sz.block + 1, lanes] = off[k : k + 1].astype(F32)
        perm_ref[:, lanes] = onehot(iota((sz.entries, c), 0) == pos[k : k + 1])
    parts = jnp.concatenate(split3(val_ref[...]), axis=0)
    moved = dot_t(parts, perm_ref[...])
    moved = moved[:height] + moved[height : 2 * height] + moved[2 * height :]
    if dots is not None:
        lane = iota((height, c), 1) & (sz.refs - 1)
        row = iota((height, c), 0)
    group = iota((sz.push_rows, c), 1) >> (sz.refs.bit_length() - 1)
    for chunk in range(sz.lists):
        x = moved[:, chunk * c : (chunk + 1) * c]
        if dots is not None:
            for at, d in enumerate(dots):
                x = jnp.where((row == sz.block + 1) & (lane == at), d, x)
        for t in range(sz.groups):
            roll_ref[t] = pltpu.roll(x, t * sz.refs, 1) if t else x
        for s in range(sz.groups):
            e = chunk * sz.groups + s
            out = jnp.zeros((sz.push_rows, c), F32)
            for g in range(-(-sz.values // sz.push_rows)):
                part = roll_ref[(g - s) % sz.groups, pl.ds(g * sz.push_rows, sz.push_rows), :]
                out = jnp.where(group == g, part, out)
            msg_ref[pl.ds(e * sz.rows, sz.block), :] = v
            msg_ref[pl.ds(e * sz.rows + sz.block, sz.push_rows), :] = out


def gather(sz, msg_ref, own, off):
    c = sz.cams
    left = jnp.concatenate(split3(msg_ref[...]), axis=1)
    period = math.lcm(sz.rows, 8)
    per = period // sz.rows
    width = 2 * c
    row = iota((period, width), 0)
    owner_at = jnp.zeros((period, width), I32)
    for q in range(1, per):
        owner_at = owner_at + jnp.where(row >= q * sz.rows, 1, 0)
    out = []
    for k in range(0, sz.lists, 2):
        pair = jnp.concatenate([off[k : k + 1], off[k + 1 : k + 2]], axis=1)
        right = onehot(iota((c, width), 0) == pair)
        res = dot(left, jnp.concatenate([right] * 3, axis=0))
        owner = jnp.concatenate([own[k : k + 1], own[k + 1 : k + 2]], axis=1) - owner_at
        acc = jnp.zeros((period, width), F32)
        for m in range(sz.devices // per):
            part = res[m * period : (m + 1) * period]
            acc = jnp.where(owner == m * per, part, acc)
        g = acc[: sz.block]
        for q in range(1, per):
            g = g + acc[q * sz.rows : q * sz.rows + sz.block]
        out += [g[:, :c], g[:, c:]]
    return out


def value_at(sz, v):
    return v // sz.push_rows, v % sz.push_rows


def scatter(sz, msg_ref, flat_ref, hot_ref):
    c = sz.cams
    pushed = [
        msg_ref[pl.ds(sz.block + r, sz.devices, stride=sz.rows), :] for r in range(sz.push_rows)
    ]
    lane_group = iota((sz.devices, c), 1) >> (sz.refs.bit_length() - 1)
    g, r = value_at(sz, sz.block)
    offs = jnp.where(lane_group == g, pushed[r], 0.0)
    step = sz.refs
    while step < c:
        offs = offs + pltpu.roll(offs, step, 1)
        step *= 2
    offs = offs.astype(I32)
    height = flat_ref.shape[0]
    masks = []
    row = iota((height, c), 0)
    group = iota((height, c), 1) >> (sz.refs.bit_length() - 1)
    for r in range(sz.push_rows):
        mask = jnp.zeros((height, c), I32)
        for v in range(sz.block):
            if v % sz.push_rows == r:
                mask = mask + jnp.where((row == v) & (group == v // sz.push_rows), 1, 0)
        masks.append(mask > 0)
    for d in range(sz.devices):
        lanes = slice(d * c, (d + 1) * c)
        tile = jnp.zeros((height, c), F32)
        for r in range(sz.push_rows):
            tile = jnp.where(masks[r], pushed[r][d : d + 1], tile)
        flat_ref[:, lanes] = tile
        hot_ref[:, lanes] = onehot(iota((c, c), 0) == offs[d : d + 1])
    parts = jnp.concatenate(split3(flat_ref[...]), axis=0)
    res = dot_t(parts, hot_ref[...])
    res = res[:height] + res[height : 2 * height] + res[2 * height :]
    return res[: sz.block]


def first_kernel(
    sz, rhs_ref, pre_ref, up_ref, cols_ref, table_ref,
    msg_ref, own_ref, off_ref, pos_ref, z_ref,
    val_ref, perm_ref, roll_ref,
):
    c = sz.cams
    cols = cols_ref[...]
    table = table_ref[...]
    height = table.shape[0]
    low = cols & (c - 1)
    high = cols >> sz.shift
    left = jnp.concatenate([table >> sz.shift, table & (c - 1)], axis=0).astype(F32).astype(BF16)
    owns, offs = [], []
    for k in range(sz.lists):
        res = dot(left, onehot(iota((c, c), 0) == low[k : k + 1]))
        here = iota((height, c), 0) == high[k : k + 1]
        owns.append(col_sum(jnp.where(here, res[:height], 0.0)))
        offs.append(col_sum(jnp.where(here, res[height:], 0.0)))
    own = jnp.concatenate(owns, axis=0).astype(I32)
    off = jnp.concatenate(offs, axis=0).astype(I32)
    own_ref[...] = own
    off_ref[...] = off

    hots = [
        jnp.where(iota((sz.devices, c), 0) == own[k : k + 1], 1.0, 0.0) for k in range(sz.lists)
    ]
    lane = iota((c, 2 * c), 1)
    before = onehot((iota((c, 2 * c), 0) < lane) | (lane >= c))
    counts = dot(jnp.concatenate(hots, axis=0).astype(BF16), before)
    base = jnp.zeros((sz.devices, c), F32)
    places = []
    for k in range(sz.lists):
        part = counts[k * sz.devices : (k + 1) * sz.devices]
        places.append(col_sum(hots[k] * (part[:, :c] + base)))
        base = base + part[:, c:]
    pos = own * sz.refs + jnp.concatenate(places, axis=0).astype(I32)
    pos_ref[...] = pos

    z = block_apply(pre_ref, rhs_ref[...], sz=sz)
    z_ref[...] = z
    push(sz, z, None, up_ref, off, pos, val_ref, perm_ref, roll_ref, msg_ref)


def second_kernel(
    sz, got_ref, rhs_ref, z_ref, own_ref, off_ref, pos_ref, diag_ref, pre_ref, up_ref,
    msg_ref, q_ref, w_ref,
    val_ref, perm_ref, roll_ref, flat_ref, hot_ref,
):
    own, off, pos = own_ref[...], off_ref[...], pos_ref[...]
    b, z = rhs_ref[...], z_ref[...]
    gathered = gather(sz, got_ref, own, off)
    pushed = scatter(sz, got_ref, flat_ref, hot_ref)
    q = block_apply(diag_ref, z, pushed, up_ref, gathered, sz)
    w = block_apply(pre_ref, q, sz=sz)
    q_ref[...] = q
    w_ref[...] = w
    dots = [total(b * z), total(z * q), total(b * w), total(q * w)]
    push(sz, w, dots, up_ref, off, pos, val_ref, perm_ref, roll_ref, msg_ref)


def third_kernel(
    sz, got_ref, rhs_ref, z_ref, q_ref, w_ref, own_ref, off_ref, diag_ref, up_ref,
    part_ref, dot_ref, sol_ref, res_ref, dir_ref, img_ref,
    flat_ref, hot_ref,
):
    own, off = own_ref[...], off_ref[...]
    b, z, q, w = rhs_ref[...], z_ref[...], q_ref[...], w_ref[...]
    gathered = gather(sz, got_ref, own, off)
    pushed = scatter(sz, got_ref, flat_ref, hot_ref)
    y = block_apply(diag_ref, w, pushed, up_ref, gathered, sz)
    g, r = value_at(sz, sz.block + 1)
    sums = col_sum(got_ref[pl.ds(sz.block + r, sz.devices, stride=sz.rows), :])
    lane = iota(sums.shape, 1)
    bz, zq, bw, qw = [
        jnp.sum(jnp.where(lane == g * sz.refs + at, sums, 0.0), axis=1, keepdims=True)
        for at in range(4)
    ]
    step = bz / zq
    new_dot = bz - step * (zq + bw) + step * step * qw
    beta = new_dot / bz
    direction = (1.0 + beta) * z - step * w
    image = (1.0 + beta) * q - step * y
    sol_ref[...] = step * z
    res_ref[...] = b - step * q
    dir_ref[...] = direction
    img_ref[...] = image
    dot_ref[...] = jnp.broadcast_to(new_dot, dot_ref.shape)
    part_ref[...] = jnp.broadcast_to(total(direction * image), part_ref.shape)


def fourth_kernel(part_ref, dot_ref, sol_ref, res_ref, dir_ref, img_ref, out_ref, left_ref):
    step = dot_ref[...] / col_sum(part_ref[...])
    out_ref[...] = sol_ref[...] + step * dir_ref[...]
    left_ref[...] = res_ref[...] - step * img_ref[...]


def call(body, name, outs, scratch, *args):
    spec = pl.BlockSpec(memory_space=pltpu.VMEM)
    return pl.pallas_call(
        body,
        name=name,
        out_shape=[jax.ShapeDtypeStruct(s, t) for s, t in outs],
        in_specs=[spec] * len(args),
        out_specs=[spec] * len(outs),
        scratch_shapes=scratch,
    )(*args)


def exchange(sz, msg, rows):
    tile = math.gcd(rows, 4)
    blocks = msg.reshape(sz.devices, rows // tile, tile, sz.cams)
    got = lax.all_to_all(blocks, "rows", split_axis=0, concat_axis=0, tiled=True)
    return got.reshape(sz.devices * rows, sz.cams)


def local(right_side, diag_blocks, precond, upper_blocks, block_cols, slot_of_camera):
    block, cams = right_side.shape
    sz = Sizes(block, block_cols.shape[0], cams, lax.axis_size("rows"))
    field = ((block, cams), F32)
    index = ((sz.lists, cams), I32)
    message = ((sz.devices * sz.rows, cams), F32)
    height = -(-max(sz.values, -(-sz.values // sz.push_rows) * sz.push_rows) // 16) * 16
    push_scratch = [
        pltpu.VMEM((height, sz.entries), F32),
        pltpu.VMEM((sz.entries, sz.entries), BF16),
        pltpu.VMEM((sz.groups, height, cams), F32),
    ]
    scatter_scratch = [
        pltpu.VMEM((16, sz.devices * cams), F32),
        pltpu.VMEM((cams, sz.devices * cams), BF16),
    ]
    table = slot_of_camera.reshape(-1, cams)
    msg, own, off, pos, z = call(
        functools.partial(first_kernel, sz), "first",
        [message, index, index, index, field], push_scratch,
        right_side, precond, upper_blocks, block_cols, table,
    )
    got = exchange(sz, msg, sz.rows)
    msg, q, w = call(
        functools.partial(second_kernel, sz), "second",
        [message, field, field], push_scratch + scatter_scratch,
        got, right_side, z, own, off, pos, diag_blocks, precond, upper_blocks,
    )
    got = exchange(sz, msg, sz.rows)
    part, new_dot, sol, res, direction, image = call(
        functools.partial(third_kernel, sz), "third",
        [((sz.devices, cams), F32), ((1, cams), F32)] + [field] * 4, scatter_scratch,
        got, right_side, z, q, w, own, off, diag_blocks, upper_blocks,
    )
    parts = exchange(sz, part, 1)
    return tuple(
        call(
            fourth_kernel, "fourth", [field, field], [],
            parts, new_dot, sol, res, direction, image,
        )
    )


def solution(mesh):
    return jax.shard_map(
        local,
        mesh=mesh,
        in_specs=(
            P(None, "rows"),
            P(None, None, "rows"),
            P(None, None, "rows"),
            P(None, None, None, "rows"),
            P(None, "rows"),
            P(),
        ),
        out_specs=(P(None, "rows"), P(None, "rows")),
        check_vma=False,
    )
```

time: 280 us -> 53.5 us (0.19)
  blocking collectives: 120 us -> 38.9 us
  local copies, waits for them, and re-layouts: 54.8 us -> 1.88 us
  matrix products: 35.5 us -> 0 us
  other arithmetic: 27.7 us -> 0 us
  starting transfers between devices: 25 us -> 0 us
  Pallas kernels: 0 us -> 11.7 us
  waiting for transfers between devices: 10.9 us -> 0 us
  between operations: 5.14 us -> 0.63 us
    psum x3 -> x0, blocking collectives: 120 us -> none  [the longest x2 81.2 us: residual_dot(): return lax.psum(jnp.sum(residual * precond_res), 'rows')]
    all_to_all x0 -> x3, blocking collectives: none -> 38.9 us  [exchange(): lax.all_to_all(blocks, 'rows', split_axis=0, concat_axis=0, tiled=True)]
    dot_general x7 -> x0, matrix products: 35.5 us -> none  [the longest x2 19.5 us: local(): jnp.einsum('kabc,bkc->ac', upper_blocks, gathered, precision=highest)]
    gather x8 -> x0, local copies, waits for them, and re-layouts: 27.5 us -> none  [the longest x1 6.15 us: local(): slot_lists = slot_of_camera[block_cols]]
    all_to_all x5 -> x0, starting transfers between devices: 25 us -> none  [the longest x2 11.3 us: local(): lax.all_to_all(outgoing, 'rows', split_axis=1, concat_axis=1, tiled=True)]
    unnamed x25 -> x1, local copies, waits for them, and re-layouts: 22.3 us -> 1.88 us
    scatter-add x2 -> x0, other arithmetic: 12.6 us -> none  [local(): result = result.at[:, requested_flat].add(pushed.reshape(BLOCK, -1))]
    pallas_call x0 -> x4, Pallas kernels: none -> 11.7 us  [call(): pl.pallas_call(body, name=name, out_shape=[jax.ShapeDtypeStruct(s, t) for...]
  transfers between devices with their start and end apart: 5 -> 0, of which waited for: 3 -> 0; matrix products, arithmetic and copies ran while one was open for 17% -> 0% of each run, Pallas kernels for 0% -> 0%
where the time goes in v1:
time: 53.5 us; the launch traced here: 53.1 us
  blocking collectives  38.9 us (73%)
  Pallas kernels  11.7 us (22%)
  local copies, waits for them, and re-layouts  1.88 us (4%)
  between operations  0.63 us (1%)
    all_to_all x3, blocking collectives, exchange(): lax.all_to_all(blocks, 'rows', split_axis=0, concat_axis=0, tiled=True)  38.9 us
    pallas_call x4, Pallas kernels, call(): pl.pallas_call(body, name=name, out_shape=[jax.ShapeDtypeStruct(s, t) for...  11.7 us
    unnamed x1, local copies, waits for them, and re-layouts  1.88 us

profile of v1, /device:TPU:0, one launch (start us, length us, event | category | flops | bytes accessed | tf_op | source)
XLA Modules:
  0.0 53.1 jit_solution(3142516878619868445)
XLA Ops:
  0.6 1.9 %copy.11.up_ref = f32[8,9,9,128]{3,2,1,0:T(8,128)} copy(f32[8,9,9,128]{3,0,2,1:T(8,128)} %param.9) | data formatting | bytes 663552 | tf_op args[3]
  2.5 3.2 %first.1 = (f32[384,128]{1,0:T(8,128)}, s32[8,128]{1,0:T(8,128)}, s32[8,128]{1,0:T(8,128)}, s32[8,128]{1,0:T(8,128)}, f32[9,128]{1,0:T(8,128)}) custom-call(f32[9,128]{1,0:T(8,128)} %rhs_ref.5, f32[9,9,128]{2,1,0:T(8,128)} %pre_ref.3, f32[8,9,9,128]{3,2,1,0:T(8,128)} %copy.11.up_ref, s32[8,128]{1,0:T(8,128)} %cols_ref.1, s32[32,128]{1,0:T(8,128)} %bitcast.14), custom_call_target="tpu_custom_call" | custom-call | tf_op jit(solution)/shard_map/first/pallas_call | solution.py:279
  5.7 16.4 %all_to_all.15 = f32[32,3,4,128]{3,2,1,0:T(4,128)} all-to-all(f32[32,3,4,128]{3,2,1,0:T(4,128)} %bitcast.11), channel_id=1, replica_groups=mesh['rows'=32] {'rows'}, dimensions={0} | all-to-all | bytes 393216 | tf_op jit(solution)/shard_map/all_to_all | solution.py:292
  22.1 4.1 %second.1 = (f32[384,128]{1,0:T(8,128)}, f32[9,128]{1,0:T(8,128)}, f32[9,128]{1,0:T(8,128)}) custom-call(f32[384,128]{1,0:T(8,128)} %bitcast.10, f32[9,128]{1,0:T(8,128)} %rhs_ref.5, f32[9,128]{1,0:T(8,128)} %get-tuple-element.17.z_ref, s32[8,128]{1,0:T(8,128)} %get-tuple-element.18.own_ref, s32[8,128]{1,0:T(8,128)} %get-tuple-element.19.off_ref, ...), custom_call_target="tpu_custom_call" | custom-call | tf_op jit(solution)/shard_map/second/pallas_call | solution.py:279
  26.2 12.2 %all_to_all.16 = f32[32,3,4,128]{3,2,1,0:T(4,128)} all-to-all(f32[32,3,4,128]{3,2,1,0:T(4,128)} %bitcast.12), channel_id=1, replica_groups=mesh['rows'=32] {'rows'}, dimensions={0} | all-to-all | bytes 393216 | tf_op jit(solution)/shard_map/all_to_all | solution.py:292
  38.5 3.0 %third.1 = (f32[32,128]{1,0:T(8,128)}, f32[1,128]{1,0:T(1,128)}, f32[9,128]{1,0:T(8,128)}, f32[9,128]{1,0:T(8,128)}, f32[9,128]{1,0:T(8,128)}, /*index=5*/f32[9,128]{1,0:T(8,128)}) custom-call(f32[384,128]{1,0:T(8,128)} %bitcast.9, f32[9,128]{1,0:T(8,128)} %rhs_ref.5, f32[9,128]{1,0:T(8,128)} %get-tuple-element.17.z_ref, f32[9,128]{1,0:T(8,128)} %get-tuple-element.22.q_ref, ...), custom_call_target="tpu_custom_call" | custom-call | tf_op jit(solution)/shard_map/third/pallas_call | solution.py:279
  41.5 10.3 %all_to_all.17 = f32[32,1,1,128]{3,2,1,0:T(1,128)} all-to-all(f32[32,1,1,128]{3,2,1,0:T(1,128)} %bitcast.15), channel_id=1, replica_groups=mesh['rows'=32] {'rows'}, dimensions={0} | all-to-all | bytes 32768 | tf_op jit(solution)/shard_map/all_to_all | solution.py:292
  51.7 1.4 %fourth.1 = (f32[9,128]{1,0:T(8,128)}, f32[9,128]{1,0:T(8,128)}) custom-call(f32[32,128]{1,0:T(8,128)} %bitcast.13, f32[1,128]{1,0:T(1,128)} %get-tuple-element.25.dot_ref, f32[9,128]{1,0:T(8,128)} %get-tuple-element.26.sol_ref, f32[9,128]{1,0:T(8,128)} %get-tuple-element.27.res_ref, f32[9,128]{1,0:T(8,128)} %get-tuple-element.28.dir_ref, ...), custom_call_target="tpu_custom_call" | custom-call | tf_op jit(solution)/shard_map/fourth/pallas_call | solution.py:279

commit v2 on v1

v2 whole, which is shorter than its diff:
```python
import functools
import math

import jax
import jax.numpy as jnp
from jax import lax
from jax.experimental import pallas as pl
from jax.experimental.pallas import tpu as pltpu
from jax.sharding import PartitionSpec as P

VMEM = 24 << 20
TALL = 16
F32 = jnp.float32
BF16 = jnp.bfloat16
I32 = jnp.int32


class Packing:
    def __init__(self, values, refs, cams, skip):
        self.refs = refs
        self.cams = cams
        self.groups = cams // refs
        self.bits = refs.bit_length() - 1
        self.values = values
        self.rows = -(-values // self.groups)
        self.skip = skip
        self.stride = skip + self.rows

    def at(self, v):
        return v // self.rows, v % self.rows

    def group(self, shape):
        return lax.broadcasted_iota(I32, shape, 1) >> self.bits

    def read(self, msg_ref, r, devices):
        return msg_ref[pl.ds(self.skip + r, devices, stride=self.stride), :]


class Sizes:
    def __init__(self, block, lists, cams, devices):
        self.block = block
        self.lists = lists
        self.cams = cams
        self.devices = devices
        self.entries = lists * cams
        self.refs = self.entries // devices
        self.shift = cams.bit_length() - 1
        assert cams == 1 << self.shift and self.refs * devices == self.entries
        assert self.refs == 1 << (self.refs.bit_length() - 1) and lists <= 8
        self.one = Packing(block + 1, self.refs, cams, block)
        self.two = Packing(2 * block + 1, self.refs, cams, 0)
        self.answer = block + 1
        assert self.answer % self.two.rows == 0


def split3(x):
    hi = x.astype(BF16)
    rest = x - hi.astype(F32)
    mid = rest.astype(BF16)
    low = (rest - mid.astype(F32)).astype(BF16)
    return hi, mid, low


def stacked(x):
    return jnp.concatenate(split3(x), axis=0)


def folded(x):
    height = x.shape[0] // 3
    return x[:height] + x[height : 2 * height] + x[2 * height :]


def dot(a, b):
    return lax.dot_general(a, b, (((1,), (0,)), ((), ())), preferred_element_type=F32)


def dot_t(a, b):
    return lax.dot_general(a, b, (((1,), (1,)), ((), ())), preferred_element_type=F32)


def iota(shape, axis):
    return lax.broadcasted_iota(I32, shape, axis)


def onehot(mask):
    return jnp.where(mask, 1.0, 0.0).astype(BF16)


def col_sum(x):
    return jnp.sum(x, axis=0, keepdims=True)


def total(x):
    return jnp.sum(col_sum(x), axis=1, keepdims=True)


def block_apply(sz, blocks_ref, v):
    return jnp.concatenate([col_sum(blocks_ref[a] * v) for a in range(sz.block)], axis=0)


def upper_apply(sz, up_ref, col_ref):
    gathered = [col_ref[pl.ds(b, sz.lists, stride=TALL), :] for b in range(sz.block)]
    rows = []
    for a in range(sz.block):
        acc = up_ref[a, 0] * gathered[0]
        for b in range(1, sz.block):
            acc = acc + up_ref[a, b] * gathered[b]
        rows.append(col_sum(acc))
    return jnp.concatenate(rows, axis=0)


def flat_lanes(sz, ref):
    return jnp.concatenate([ref[k * TALL : (k + 1) * TALL, :] for k in range(sz.lists)], axis=1)


def bucketed(sz, v, off, up_ref, perm_ref, val_ref):
    val_ref[...] = jnp.zeros_like(val_ref)
    for b in range(sz.block):
        acc = up_ref[0, b] * v[0:1]
        for a in range(1, sz.block):
            acc = acc + up_ref[a, b] * v[a : a + 1]
        val_ref[pl.ds(b, sz.lists, stride=TALL), :] = acc
    if off is not None:
        val_ref[pl.ds(sz.block, sz.lists, stride=TALL), :] = off.astype(F32)
    return folded(dot_t(stacked(flat_lanes(sz, val_ref)), perm_ref[...]))


def packed(sz, pk, values, x, roll_ref):
    group = pk.group((pk.rows, sz.cams))
    for t in range(pk.groups):
        roll_ref[t] = pltpu.roll(x, t * sz.refs, 1) if t else x
    for s in range(pk.groups):
        out = jnp.zeros((pk.rows, sz.cams), F32)
        for g in range(-(-values // pk.rows)):
            part = roll_ref[(g - s) % pk.groups, pl.ds(g * pk.rows, pk.rows), :]
            out = jnp.where(group == g, part, out)
        yield s, out


def scatter(sz, pk, msg_ref, flat_ref, hot_ref, offsets):
    c = sz.cams
    pushed = [pk.read(msg_ref, r, sz.devices) for r in range(pk.rows)]
    if offsets:
        g, r = pk.at(sz.block)
        offs = jnp.where(pk.group((sz.devices, c)) == g, pushed[r], 0.0)
        step = sz.refs
        while step < c:
            offs = offs + pltpu.roll(offs, step, 1)
            step *= 2
        offs = offs.astype(I32)
    row = iota((TALL, c), 0)
    group = pk.group((TALL, c))
    masks = []
    for r in range(pk.rows):
        mask = jnp.zeros((TALL, c), I32)
        for v in range(sz.block):
            if v % pk.rows == r:
                mask = mask + jnp.where((row == v) & (group == v // pk.rows), 1, 0)
        masks.append(mask > 0)
    for d in range(sz.devices):
        lanes = slice(d * c, (d + 1) * c)
        tile = jnp.zeros((TALL, c), F32)
        for r in range(pk.rows):
            tile = jnp.where(masks[r], pushed[r][d : d + 1], tile)
        flat_ref[:, lanes] = tile
        if offsets:
            hot_ref[:, lanes] = onehot(iota((c, c), 0) == offs[d : d + 1])
    return folded(dot_t(stacked(flat_ref[...]), hot_ref[...]))[: sz.block]


def gather(sz, msg_ref, own, off, col_ref):
    c = sz.cams
    rows = sz.one.stride
    left = jnp.concatenate(split3(msg_ref[...]), axis=1)
    period = math.lcm(rows, 8)
    per = period // rows
    width = 2 * c
    row = iota((period, width), 0)
    owner_at = jnp.zeros((period, width), I32)
    for q in range(1, per):
        owner_at = owner_at + jnp.where(row >= q * rows, 1, 0)
    for k in range(0, sz.lists, 2):
        pair = jnp.concatenate([off[k : k + 1], off[k + 1 : k + 2]], axis=1)
        right = onehot(iota((c, width), 0) == pair)
        res = dot(left, jnp.concatenate([right] * 3, axis=0))
        owner = jnp.concatenate([own[k : k + 1], own[k + 1 : k + 2]], axis=1) - owner_at
        acc = jnp.zeros((period, width), F32)
        for m in range(sz.devices // per):
            acc = jnp.where(owner == m * per, res[m * period : (m + 1) * period], acc)
        g = acc[: sz.block]
        for q in range(1, per):
            g = g + acc[q * rows : q * rows + sz.block]
        col_ref[pl.ds(k * TALL, sz.block), :] = g[:, :c]
        col_ref[pl.ds((k + 1) * TALL, sz.block), :] = g[:, c:]


def unpack_answers(sz, msg_ref, perm_ref, turn_ref, val_ref, col_ref):
    pk, c = sz.two, sz.cams
    for r in range(pk.rows):
        x = pk.read(msg_ref, r, sz.devices)
        for t in range(pk.groups):
            turn_ref[r, t] = pltpu.roll(x, t * sz.refs, 1) if t else x
    group = pk.group((sz.lists, c))
    val_ref[...] = jnp.zeros_like(val_ref)
    for b in range(sz.block):
        g, r = pk.at(sz.answer + b)
        out = jnp.zeros((sz.lists, c), F32)
        for s in range(pk.groups):
            part = turn_ref[r, (s - g) % pk.groups, pl.ds(s, sz.lists, stride=pk.groups), :]
            out = jnp.where(group == s, part, out)
        val_ref[pl.ds(b, sz.lists, stride=TALL), :] = out
    res = folded(dot(stacked(flat_lanes(sz, val_ref)), perm_ref[...]))
    for k in range(sz.lists):
        col_ref[k * TALL : (k + 1) * TALL, :] = res[:, k * c : (k + 1) * c]


def first_kernel(
    sz, cols_hbm, table_hbm, rhs_hbm, pre_hbm, up_hbm, diag_hbm,
    msg_ref, own_ref, off_ref, z_ref, perm_ref, rhs_ref, pre_ref, up_ref, diag_ref,
    cols_ref, table_ref, val_ref, roll_ref, sems,
):
    pairs = (
        (cols_hbm, cols_ref), (table_hbm, table_ref), (rhs_hbm, rhs_ref), (pre_hbm, pre_ref),
        (up_hbm, up_ref), (diag_hbm, diag_ref),
    )
    copies = [pltpu.make_async_copy(a, b, sems.at[i]) for i, (a, b) in enumerate(pairs)]
    for copy in copies:
        copy.start()
    copies[0].wait()
    copies[1].wait()
    c = sz.cams
    cols = cols_ref[...]
    table = table_ref[...]
    height = table.shape[0]
    low = cols & (c - 1)
    high = cols >> sz.shift
    left = jnp.concatenate([table >> sz.shift, table & (c - 1)], axis=0).astype(F32).astype(BF16)
    owns, offs = [], []
    for k in range(sz.lists):
        res = dot(left, onehot(iota((c, c), 0) == low[k : k + 1]))
        here = iota((height, c), 0) == high[k : k + 1]
        owns.append(col_sum(jnp.where(here, res[:height], 0.0)))
        offs.append(col_sum(jnp.where(here, res[height:], 0.0)))
    own = jnp.concatenate(owns, axis=0).astype(I32)
    off = jnp.concatenate(offs, axis=0).astype(I32)
    own_ref[...] = own
    off_ref[...] = off

    hots = [
        jnp.where(iota((sz.devices, c), 0) == own[k : k + 1], 1.0, 0.0) for k in range(sz.lists)
    ]
    lane = iota((c, 2 * c), 1)
    before = onehot((iota((c, 2 * c), 0) < lane) | (lane >= c))
    counts = dot(jnp.concatenate(hots, axis=0).astype(BF16), before)
    base = jnp.zeros((sz.devices, c), F32)
    for k in range(sz.lists):
        part = counts[k * sz.devices : (k + 1) * sz.devices]
        place = col_sum(hots[k] * (part[:, :c] + base)).astype(I32)
        base = base + part[:, c:]
        pos = own[k : k + 1] * sz.refs + place
        perm_ref[:, k * c : (k + 1) * c] = onehot(iota((sz.entries, c), 0) == pos)

    copies[2].wait()
    copies[3].wait()
    z = block_apply(sz, pre_ref, rhs_ref[...])
    z_ref[...] = z
    copies[4].wait()
    moved = bucketed(sz, z, off, up_ref, perm_ref, val_ref)
    pk = sz.one
    for chunk in range(sz.lists):
        x = moved[:, chunk * c : (chunk + 1) * c]
        for s, out in packed(sz, pk, pk.values, x, roll_ref):
            e = chunk * pk.groups + s
            msg_ref[pl.ds(e * pk.stride, sz.block), :] = z
            msg_ref[pl.ds(e * pk.stride + sz.block, pk.rows), :] = out
    copies[5].wait()


def second_kernel(
    sz, got_ref, rhs_ref, z_ref, own_ref, off_ref, perm_ref, diag_ref, pre_ref, up_ref,
    msg_ref, q_ref, w_ref, hot_ref,
    val_ref, roll_ref, flat_ref, col_ref, ans_ref,
):
    c, pk = sz.cams, sz.two
    b, z = rhs_ref[...], z_ref[...]
    gather(sz, got_ref, own_ref[...], off_ref[...], col_ref)
    pushed = scatter(sz, sz.one, got_ref, flat_ref, hot_ref, True)
    q = block_apply(sz, diag_ref, z) + upper_apply(sz, up_ref, col_ref) + pushed
    w = block_apply(sz, pre_ref, q)
    q_ref[...] = q
    w_ref[...] = w
    dots = [total(b * z), total(z * q), total(b * w), total(q * w)]
    lane = iota((1, c), 1) & (sz.refs - 1)
    dot_row = jnp.zeros((1, c), F32)
    for at, d in enumerate(dots):
        dot_row = jnp.where(lane == at, d, dot_row)
    tall = jnp.concatenate([w, jnp.zeros((TALL - sz.block, c), F32)], axis=0)
    ans_ref[...] = folded(dot(stacked(tall), hot_ref[...]))
    moved = bucketed(sz, w, None, up_ref, perm_ref, val_ref)
    row = iota((TALL, c), 0)
    group = pk.group((pk.rows, c))
    first = sz.answer // pk.rows
    for chunk in range(sz.lists):
        x = jnp.where(row == sz.block, dot_row, moved[:, chunk * c : (chunk + 1) * c])
        for s, out in packed(sz, pk, sz.answer, x, roll_ref):
            e = chunk * pk.groups + s
            for g in range(-(-sz.block // pk.rows)):
                part = ans_ref[pl.ds(g * pk.rows, pk.rows), e * c : (e + 1) * c]
                out = jnp.where(group == first + g, part, out)
            msg_ref[pl.ds(e * pk.stride, pk.rows), :] = out


def third_kernel(
    sz, got_ref, rhs_ref, z_ref, q_ref, w_ref, perm_ref, hot_ref, diag_ref, up_ref,
    part_ref, dot_ref, sol_ref, res_ref, dir_ref, img_ref,
    val_ref, turn_ref, flat_ref, col_ref,
):
    pk = sz.two
    b, z, q, w = rhs_ref[...], z_ref[...], q_ref[...], w_ref[...]
    unpack_answers(sz, got_ref, perm_ref, turn_ref, val_ref, col_ref)
    pushed = scatter(sz, pk, got_ref, flat_ref, hot_ref, False)
    y = block_apply(sz, diag_ref, w) + upper_apply(sz, up_ref, col_ref) + pushed
    g, r = pk.at(sz.block)
    sums = col_sum(pk.read(got_ref, r, sz.devices))
    lane = iota(sums.shape, 1)
    bz, zq, bw, qw = [
        jnp.sum(jnp.where(lane == g * sz.refs + at, sums, 0.0), axis=1, keepdims=True)
        for at in range(4)
    ]
    step = bz / zq
    new_dot = bz - step * (zq + bw) + step * step * qw
    beta = new_dot / bz
    direction = (1.0 + beta) * z - step * w
    image = (1.0 + beta) * q - step * y
    sol_ref[...] = step * z
    res_ref[...] = b - step * q
    dir_ref[...] = direction
    img_ref[...] = image
    dot_ref[...] = jnp.broadcast_to(new_dot, dot_ref.shape)
    part_ref[...] = jnp.broadcast_to(total(direction * image), part_ref.shape)


def fourth_kernel(part_ref, dot_ref, sol_ref, res_ref, dir_ref, img_ref, out_ref, left_ref):
    step = dot_ref[...] / col_sum(part_ref[...])
    out_ref[...] = sol_ref[...] + step * dir_ref[...]
    left_ref[...] = res_ref[...] - step * img_ref[...]


def call(body, name, outs, scratch, *args, space=pltpu.VMEM):
    return pl.pallas_call(
        body,
        name=name,
        out_shape=[jax.ShapeDtypeStruct(s, t) for s, t in outs],
        in_specs=[pl.BlockSpec(memory_space=space)] * len(args),
        out_specs=[pl.BlockSpec(memory_space=pltpu.VMEM)] * len(outs),
        scratch_shapes=scratch,
        compiler_params=pltpu.CompilerParams(vmem_limit_bytes=VMEM),
    )(*args)


def exchange(sz, msg, rows):
    tile = math.gcd(rows, 4)
    blocks = msg.reshape(sz.devices, rows // tile, tile, sz.cams)
    got = lax.all_to_all(blocks, "rows", split_axis=0, concat_axis=0, tiled=True)
    return got.reshape(sz.devices * rows, sz.cams)


def local(right_side, diag_blocks, precond, upper_blocks, block_cols, slot_of_camera):
    block, cams = right_side.shape
    lists = block_cols.shape[0]
    sz = Sizes(block, lists, cams, lax.axis_size("rows"))
    field = ((block, cams), F32)
    index = ((lists, cams), I32)
    perm_type = ((sz.entries, sz.entries), BF16)
    wide = sz.devices * cams
    upper_blocks = upper_blocks.transpose(1, 2, 0, 3)
    table = slot_of_camera.reshape(-1, cams)
    values = pltpu.VMEM((lists * TALL, cams), F32)
    flat = pltpu.VMEM((TALL, wide), F32)

    def rolls(pk):
        return pltpu.VMEM((pk.groups, TALL, cams), F32)

    ins = (block_cols, table, right_side, precond, upper_blocks, diag_blocks)
    msg, own, off, z, perm, right_side, precond, upper_blocks, diag_blocks = call(
        functools.partial(first_kernel, sz), "first",
        [((sz.devices * sz.one.stride, cams), F32), index, index, field, perm_type]
        + [(x.shape, x.dtype) for x in ins[2:]],
        [pltpu.VMEM(x.shape, x.dtype) for x in ins[:2]]
        + [values, rolls(sz.one), pltpu.SemaphoreType.DMA((len(ins),))],
        *(pltpu.with_memory_space_constraint(x, pltpu.HBM) for x in ins), space=pltpu.HBM,
    )
    got = exchange(sz, msg, sz.one.stride)
    msg, q, w, hot = call(
        functools.partial(second_kernel, sz), "second",
        [((sz.devices * sz.two.stride, cams), F32), field, field, ((cams, wide), BF16)],
        [values, rolls(sz.two), flat, values, flat],
        got, right_side, z, own, off, perm, diag_blocks, precond, upper_blocks,
    )
    got = exchange(sz, msg, sz.two.stride)
    part, new_dot, sol, res, direction, image = call(
        functools.partial(third_kernel, sz), "third",
        [((sz.devices, cams), F32), ((1, cams), F32)] + [field] * 4,
        [values, pltpu.VMEM((sz.two.rows, sz.two.groups, sz.devices, cams), F32), flat, values],
        got, right_side, z, q, w, perm, hot, diag_blocks, upper_blocks,
    )
    parts = exchange(sz, part, 1)
    return tuple(
        call(
            fourth_kernel, "fourth", [field, field], [],
            parts, new_dot, sol, res, direction, image,
        )
    )


def solution(mesh):
    return jax.shard_map(
        local,
        mesh=mesh,
        in_specs=(
            P(None, "rows"),
            P(None, None, "rows"),
            P(None, None, "rows"),
            P(None, None, None, "rows"),
            P(None, "rows"),
            P(),
        ),
        out_specs=(P(None, "rows"), P(None, "rows")),
        check_vma=False,
    )
```

time: 53.5 us -> 42.8 us (0.80)
  Pallas kernels: 11.7 us -> 7.02 us
  blocking collectives: 38.9 us -> 34.9 us
  local copies, waits for them, and re-layouts: 1.88 us -> 0 us
    pallas_call x4, Pallas kernels: 11.7 us -> 7.02 us  [call(): pl.pallas_call(body, name=name, out_shape=[jax.ShapeDtypeStruct(s, t) for...]
    all_to_all x3, blocking collectives: 38.9 us -> 34.9 us  [exchange(): lax.all_to_all(blocks, 'rows', split_axis=0, concat_axis=0, tiled=True)]
    unnamed x1 -> x0, local copies, waits for them, and re-layouts: 1.88 us -> none
where the time goes in v2:
time: 42.8 us; the launch traced here: 42.6 us
  blocking collectives  34.9 us (82%)
  Pallas kernels  7.02 us (16%)
  between operations  0.65 us (2%)
    all_to_all x3, blocking collectives, exchange(): lax.all_to_all(blocks, 'rows', split_axis=0, concat_axis=0, tiled=True)  34.9 us
    pallas_call x4, Pallas kernels, call(): pl.pallas_call(body, name=name, out_shape=[jax.ShapeDtypeStruct(s, t) for...  7.02 us

profile of v2, /device:TPU:0, one launch (start us, length us, event | category | flops | bytes accessed | tf_op | source)
XLA Modules:
  0.0 42.6 jit_solution(14807373579428958850)
XLA Ops:
  0.6 3.3 %first.1 = (f32[384,128]{1,0:T(8,128)S(1)}, s32[8,128]{1,0:T(8,128)S(1)}, s32[8,128]{1,0:T(8,128)S(1)}, f32[9,128]{1,0:T(8,128)S(1)}, bf16[1024,1024]{1,0:T(8,12...) custom-call(s32[8,128]{1,0:T(8,128)} %cols_hbm.1, ...), custom_call_target="tpu_custom_call" | custom-call | tf_op jit(solution)/shard_map/first/pallas_call | solution.py:350
  3.9 16.1 %all_to_all.15 = f32[32,3,4,128]{3,2,1,0:T(4,128)S(1)} all-to-all(f32[32,3,4,128]{3,2,1,0:T(4,128)S(1)} %bitcast.12), channel_id=1, replica_groups=mesh['rows'=32] {'rows'}, dimensions={0} | all-to-all | bytes 393216 | tf_op jit(solution)/shard_map/all_to_all | solution.py:364
  20.0 2.1 %second.1 = (f32[160,128]{1,0:T(8,128)S(1)}, f32[9,128]{1,0:T(8,128)S(1)}, f32[9,128]{1,0:T(8,128)S(1)}, bf16[128,4096]{1,0:T(8,128)(2,1)S(1)}) custom-call(f32[384,128]{1,0:T(8,128)S(1)} %bitcast.10, f32[9,128]{1,0:T(8,128)S(1)} %get-tuple-element.22.rhs_ref, f32[9,128]{1,0:T(8,128)S(1)} %get-tuple-element.23.z_ref, ...), custom_call_target="tpu_custom_call" | custom-call | tf_op jit(solution)/shard_map/second/pallas_call | solution.py:350
  22.1 10.0 %all_to_all.16 = f32[32,5,1,128]{3,2,1,0:T(1,128)S(1)} all-to-all(f32[32,5,1,128]{3,2,1,0:T(1,128)S(1)} %bitcast.13), channel_id=1, replica_groups=mesh['rows'=32] {'rows'}, dimensions={0} | all-to-all | bytes 163840 | tf_op jit(solution)/shard_map/all_to_all | solution.py:364
  32.1 1.0 %third.1 = (f32[32,128]{1,0:T(8,128)S(1)}, f32[1,128]{1,0:T(1,128)S(1)}, f32[9,128]{1,0:T(8,128)S(1)}, f32[9,128]{1,0:T(8,128)S(1)}, f32[9,128]{1,0:T(8,128)S(1)}, /*index=5*/f32[9,128]{1,0:T(8,128)S(1)}) custom-call(f32[160,128]{1,0:T(8,128)S(1)} %bitcast.11, f32[9,128]{1,0:T(8,128)S(1)} %get-tuple-element.22.rhs_ref, ...), custom_call_target="tpu_custom_call" | custom-call | tf_op jit(solution)/shard_map/third/pallas_call | solution.py:350
  33.1 8.9 %all_to_all.17 = f32[32,1,1,128]{3,2,1,0:T(1,128)S(1)} all-to-all(f32[32,1,1,128]{3,2,1,0:T(1,128)S(1)} %bitcast.15), channel_id=1, replica_groups=mesh['rows'=32] {'rows'}, dimensions={0} | all-to-all | bytes 32768 | tf_op jit(solution)/shard_map/all_to_all | solution.py:364
  42.0 0.6 %fourth.1 = (f32[9,128]{1,0:T(8,128)}, f32[9,128]{1,0:T(8,128)}) custom-call(f32[32,128]{1,0:T(8,128)S(1)} %bitcast.14, f32[1,128]{1,0:T(1,128)S(1)} %get-tuple-element.35.dot_ref, f32[9,128]{1,0:T(8,128)S(1)} %get-tuple-element.36.sol_ref, f32[9,128]{1,0:T(8,128)S(1)} %get-tuple-element.37.res_ref, f32[9,128]{1,0:T(8,128)S(1)} %get-tuple-element.38.dir_ref, ...), custom_call_target="tpu_custom_call" | custom-call | tf_op jit(solution)/shard_map/fourth/pallas_call | solution.py:350

commit v3 on v2

v3 whole, which is shorter than its diff:
```python
import functools
import math

import jax
import jax.numpy as jnp
from jax import lax
from jax.experimental import pallas as pl
from jax.experimental.pallas import tpu as pltpu
from jax.sharding import PartitionSpec as P

VMEM = 24 << 20
TALL = 16
F32 = jnp.float32
BF16 = jnp.bfloat16
I32 = jnp.int32


class Packing:
    def __init__(self, values, refs, cams, skip):
        self.refs = refs
        self.cams = cams
        self.groups = cams // refs
        self.bits = refs.bit_length() - 1
        self.values = values
        self.rows = -(-values // self.groups)
        self.skip = skip
        self.stride = skip + self.rows

    def at(self, v):
        return v // self.rows, v % self.rows

    def group(self, shape):
        return lax.broadcasted_iota(I32, shape, 1) >> self.bits

    def read(self, msg_ref, r, devices):
        return msg_ref[pl.ds(self.skip + r, devices, stride=self.stride), :]


class Sizes:
    def __init__(self, block, lists, cams, devices):
        self.block = block
        self.lists = lists
        self.cams = cams
        self.devices = devices
        self.entries = lists * cams
        self.refs = self.entries // devices
        self.shift = cams.bit_length() - 1
        assert cams == 1 << self.shift and self.refs * devices == self.entries
        assert self.refs == 1 << (self.refs.bit_length() - 1) and lists <= 8
        self.one = Packing(block + 1, self.refs, cams, block)
        self.two = Packing(2 * block + 1, self.refs, cams, 0)
        self.answer = block + 1
        assert self.answer % self.two.rows == 0


def split3(x):
    hi = x.astype(BF16)
    rest = x - hi.astype(F32)
    mid = rest.astype(BF16)
    low = (rest - mid.astype(F32)).astype(BF16)
    return hi, mid, low


def stacked(x):
    return jnp.concatenate(split3(x), axis=0)


def folded(x):
    height = x.shape[0] // 3
    return x[:height] + x[height : 2 * height] + x[2 * height :]


def dot(a, b):
    return lax.dot_general(a, b, (((1,), (0,)), ((), ())), preferred_element_type=F32)


def dot_t(a, b):
    return lax.dot_general(a, b, (((1,), (1,)), ((), ())), preferred_element_type=F32)


def iota(shape, axis):
    return lax.broadcasted_iota(I32, shape, axis)


def onehot(mask):
    return jnp.where(mask, 1.0, 0.0).astype(BF16)


def hot_rows(places, shape):
    rows = iota(shape, 0).astype(F32).astype(BF16)
    same = rows == jnp.broadcast_to(places.astype(F32).astype(BF16), shape)
    return jnp.where(same, jnp.ones(shape, BF16), jnp.zeros(shape, BF16))


def col_sum(x):
    return jnp.sum(x, axis=0, keepdims=True)


def total(x):
    return jnp.sum(col_sum(x), axis=1, keepdims=True)


def block_apply(sz, blocks_ref, v):
    return jnp.concatenate([col_sum(blocks_ref[a] * v) for a in range(sz.block)], axis=0)


def upper_apply(sz, up_ref, col_ref):
    gathered = [col_ref[pl.ds(b, sz.lists, stride=TALL), :] for b in range(sz.block)]
    rows = []
    for a in range(sz.block):
        acc = up_ref[a, 0] * gathered[0]
        for b in range(1, sz.block):
            acc = acc + up_ref[a, b] * gathered[b]
        rows.append(col_sum(acc))
    return jnp.concatenate(rows, axis=0)


def side_by_side(ref, height):
    blocks = [ref[at : at + height, :] for at in range(0, ref.shape[0], height)]
    return jnp.concatenate(blocks, axis=1)


def bucketed(sz, v, off, up_ref, chunk, lane_ref, val_ref):
    for b in range(sz.block):
        acc = up_ref[0, b] * v[0:1]
        for a in range(1, sz.block):
            acc = acc + up_ref[a, b] * v[a : a + 1]
        val_ref[pl.ds(b, sz.lists, stride=TALL), :] = acc
    if off is not None:
        val_ref[pl.ds(sz.block, sz.lists, stride=TALL), :] = off.astype(F32)
    parts = stacked(side_by_side(val_ref, TALL))
    where = jnp.concatenate([chunk[k : k + 1] for k in range(sz.lists)], axis=1)
    where = jnp.broadcast_to(where.astype(F32).astype(BF16), parts.shape)
    left = [
        jnp.where(where == jnp.full(parts.shape, at, BF16), parts, jnp.zeros(parts.shape, BF16))
        for at in range(sz.lists)
    ]
    res = dot_t(jnp.concatenate(left, axis=0), side_by_side(lane_ref, sz.cams))
    return [folded(res[at * 3 * TALL : (at + 1) * 3 * TALL]) for at in range(sz.lists)]


def pack(sz, pk, value_of, msg_ref):
    group = pk.group((sz.lists, sz.cams))
    values = [value_of(v) for v in range(pk.values)]
    turned = [
        [pltpu.roll(x, t * sz.refs, 1) if t else x for t in range(pk.groups)] for x in values
    ]
    for s in range(pk.groups):
        for r in range(pk.rows):
            out = jnp.zeros((sz.lists, sz.cams), F32)
            for g in range(pk.groups):
                v = g * pk.rows + r
                if v < pk.values:
                    out = jnp.where(group == g, turned[v][(g - s) % pk.groups], out)
            at = pl.ds(s * pk.stride + pk.skip + r, sz.lists, stride=pk.groups * pk.stride)
            msg_ref[at, :] = out


def unpack(sz, pk, msg_ref, turn_ref):
    for r in range(pk.rows):
        x = pk.read(msg_ref, r, sz.devices)
        for t in range(pk.groups):
            turn_ref[r, t] = pltpu.roll(x, t * sz.refs, 1) if t else x
    group = pk.group((sz.lists, sz.cams))
    out = []
    for v in range(pk.values):
        g, r = pk.at(v)
        value = None
        for s in range(pk.groups):
            part = turn_ref[r, (s - g) % pk.groups, pl.ds(s, sz.lists, stride=pk.groups), :]
            value = part if value is None else jnp.where(group == s, part, value)
        out.append(value)
    return out


def scatter(sz, values, tall_ref, hot_ref):
    for b in range(sz.block):
        tall_ref[pl.ds(b, sz.lists, stride=TALL), :] = values[b]
    parts = stacked(side_by_side(tall_ref, TALL))
    return folded(dot_t(parts, side_by_side(hot_ref, sz.cams)))[: sz.block]


def gather(sz, msg_ref, own, off, col_ref):
    c = sz.cams
    rows = sz.one.stride
    left = jnp.concatenate(split3(msg_ref[...]), axis=1)
    period = math.lcm(rows, 8)
    per = period // rows
    width = 2 * c
    row = iota((period, width), 0)
    owner_at = jnp.zeros((period, width), I32)
    for q in range(1, per):
        owner_at = owner_at + jnp.where(row >= q * rows, 1, 0)
    for k in range(0, sz.lists, 2):
        pair = jnp.concatenate([off[k : k + 1], off[k + 1 : k + 2]], axis=1)
        right = hot_rows(pair, (c, width))
        res = dot(left, jnp.concatenate([right] * 3, axis=0))
        owner = jnp.concatenate([own[k : k + 1], own[k + 1 : k + 2]], axis=1) - owner_at
        acc = jnp.zeros((period, width), F32)
        for m in range(sz.devices // per):
            acc = jnp.where(owner == m * per, res[m * period : (m + 1) * period], acc)
        g = acc[: sz.block]
        for q in range(1, per):
            g = g + acc[q * rows : q * rows + sz.block]
        col_ref[pl.ds(k * TALL, sz.block), :] = g[:, :c]
        col_ref[pl.ds((k + 1) * TALL, sz.block), :] = g[:, c:]


def to_lists(sz, values, chunk, lane_ref, tall_ref, col_ref):
    for b in range(sz.block):
        tall_ref[pl.ds(b, sz.lists, stride=TALL), :] = values[b]
    left = jnp.concatenate(split3(tall_ref[...]), axis=1)
    right = jnp.concatenate([side_by_side(lane_ref, sz.cams)] * 3, axis=0)
    res = dot(left, right)
    for k in range(sz.lists):
        lanes = slice(k * sz.cams, (k + 1) * sz.cams)
        out = res[:TALL, lanes]
        for at in range(1, sz.lists):
            out = jnp.where(chunk[k : k + 1] == at, res[at * TALL : (at + 1) * TALL, lanes], out)
        col_ref[k * TALL : (k + 1) * TALL, :] = out


def first_kernel(
    sz, cols_hbm, table_hbm, rhs_hbm, pre_hbm, up_hbm, diag_hbm,
    msg_ref, own_ref, off_ref, chunk_ref, z_ref, lane_ref, rhs_ref, pre_ref, up_ref, diag_ref,
    cols_ref, table_ref, val_ref, tall_ref, sems,
):
    pairs = (
        (cols_hbm, cols_ref), (table_hbm, table_ref), (rhs_hbm, rhs_ref), (pre_hbm, pre_ref),
        (up_hbm, up_ref), (diag_hbm, diag_ref),
    )
    copies = [pltpu.make_async_copy(a, b, sems.at[i]) for i, (a, b) in enumerate(pairs)]
    for copy in copies:
        copy.start()
    copies[0].wait()
    copies[1].wait()
    c = sz.cams
    cols = cols_ref[...]
    table = table_ref[...]
    height = table.shape[0]
    low = cols & (c - 1)
    high = cols >> sz.shift
    left = jnp.concatenate([table >> sz.shift, table & (c - 1)], axis=0).astype(F32).astype(BF16)
    owns, offs = [], []
    for k in range(sz.lists):
        res = dot(left, hot_rows(low[k : k + 1], (c, c)))
        here = iota((height, c), 0) == high[k : k + 1]
        owns.append(col_sum(jnp.where(here, res[:height], 0.0)))
        offs.append(col_sum(jnp.where(here, res[height:], 0.0)))
    own = jnp.concatenate(owns, axis=0).astype(I32)
    off = jnp.concatenate(offs, axis=0).astype(I32)
    own_ref[...] = own
    off_ref[...] = off

    hots = [
        jnp.where(iota((sz.devices, c), 0) == own[k : k + 1], 1.0, 0.0) for k in range(sz.lists)
    ]
    lane = iota((c, 2 * c), 1)
    before = onehot((iota((c, 2 * c), 0) < lane) | (lane >= c))
    counts = dot(jnp.concatenate(hots, axis=0).astype(BF16), before)
    base = jnp.zeros((sz.devices, c), F32)
    places = []
    for k in range(sz.lists):
        part = counts[k * sz.devices : (k + 1) * sz.devices]
        places.append(col_sum(hots[k] * (part[:, :c] + base)))
        base = base + part[:, c:]
    pos = own * sz.refs + jnp.concatenate(places, axis=0).astype(I32)
    chunk = pos >> sz.shift
    place = pos & (c - 1)
    chunk_ref[...] = chunk
    for k in range(sz.lists):
        lane_ref[k * c : (k + 1) * c, :] = hot_rows(place[k : k + 1], (c, c))

    for copy in copies[2:]:
        copy.wait()
    pk = sz.one
    z = block_apply(sz, pre_ref, rhs_ref[...])
    z_ref[...] = z
    for b in range(sz.block):
        at = pl.ds(b, sz.devices, stride=pk.stride)
        msg_ref[at, :] = jnp.broadcast_to(z[b : b + 1], (sz.devices, c))
    for at, x in enumerate(bucketed(sz, z, off, up_ref, chunk, lane_ref, val_ref)):
        tall_ref[at * TALL : (at + 1) * TALL, :] = x
    pack(sz, pk, lambda v: tall_ref[pl.ds(v, sz.lists, stride=TALL), :], msg_ref)


def second_kernel(
    sz, got_ref, rhs_ref, z_ref, own_ref, off_ref, chunk_ref, lane_ref, diag_ref, pre_ref, up_ref,
    msg_ref, q_ref, w_ref, hot_ref,
    val_ref, tall_ref, ans_ref, col_ref, turn_ref,
):
    c = sz.cams
    b, z = rhs_ref[...], z_ref[...]
    values = unpack(sz, sz.one, got_ref, turn_ref)
    wanted = values[sz.block].astype(I32)
    for at in range(sz.lists):
        hot_ref[at * c : (at + 1) * c, :] = hot_rows(wanted[at : at + 1], (c, c))
    pushed = scatter(sz, values, val_ref, hot_ref)
    gather(sz, got_ref, own_ref[...], off_ref[...], col_ref)
    q = block_apply(sz, diag_ref, z) + upper_apply(sz, up_ref, col_ref) + pushed
    w = block_apply(sz, pre_ref, q)
    q_ref[...] = q
    w_ref[...] = w
    dots = [total(b * z), total(z * q), total(b * w), total(q * w)]
    lane = iota((sz.lists, c), 1) & (sz.refs - 1)
    dot_rows = jnp.zeros((sz.lists, c), F32)
    for at, d in enumerate(dots):
        dot_rows = jnp.where(lane == at, d, dot_rows)
    tall = jnp.concatenate([w, jnp.zeros((TALL - sz.block, c), F32)], axis=0)
    answers = folded(dot(stacked(tall), side_by_side(hot_ref, c)))
    for at in range(sz.lists):
        ans_ref[at * TALL : (at + 1) * TALL, :] = answers[:, at * c : (at + 1) * c]
    for at, x in enumerate(bucketed(sz, w, None, up_ref, chunk_ref[...], lane_ref, val_ref)):
        tall_ref[at * TALL : (at + 1) * TALL, :] = x

    def value_of(v):
        if v < sz.block:
            return tall_ref[pl.ds(v, sz.lists, stride=TALL), :]
        if v == sz.block:
            return dot_rows
        return ans_ref[pl.ds(v - sz.answer, sz.lists, stride=TALL), :]

    pack(sz, sz.two, value_of, msg_ref)


def third_kernel(
    sz, got_ref, rhs_ref, z_ref, q_ref, w_ref, chunk_ref, lane_ref, hot_ref, diag_ref, up_ref,
    part_ref, dot_ref, sol_ref, res_ref, dir_ref, img_ref,
    val_ref, tall_ref, col_ref, turn_ref,
):
    b, z, q, w = rhs_ref[...], z_ref[...], q_ref[...], w_ref[...]
    values = unpack(sz, sz.two, got_ref, turn_ref)
    to_lists(sz, values[sz.answer :], chunk_ref[...], lane_ref, tall_ref, col_ref)
    pushed = scatter(sz, values, val_ref, hot_ref)
    y = block_apply(sz, diag_ref, w) + upper_apply(sz, up_ref, col_ref) + pushed
    sums = col_sum(values[sz.block])
    lane = iota(sums.shape, 1) & (sz.refs - 1)
    bz, zq, bw, qw = [
        jnp.sum(jnp.where(lane == at, sums, 0.0), axis=1, keepdims=True) for at in range(4)
    ]
    step = bz / zq
    new_dot = bz - step * (zq + bw) + step * step * qw
    beta = new_dot / bz
    direction = (1.0 + beta) * z - step * w
    image = (1.0 + beta) * q - step * y
    sol_ref[...] = step * z
    res_ref[...] = b - step * q
    dir_ref[...] = direction
    img_ref[...] = image
    dot_ref[...] = jnp.broadcast_to(new_dot, dot_ref.shape)
    part_ref[...] = jnp.broadcast_to(total(direction * image), part_ref.shape)


def fourth_kernel(part_ref, dot_ref, sol_ref, res_ref, dir_ref, img_ref, out_ref, left_ref):
    step = dot_ref[...] / col_sum(part_ref[...])
    out_ref[...] = sol_ref[...] + step * dir_ref[...]
    left_ref[...] = res_ref[...] - step * img_ref[...]


def call(body, name, outs, scratch, *args, space=pltpu.VMEM):
    return pl.pallas_call(
        body,
        name=name,
        out_shape=[jax.ShapeDtypeStruct(s, t) for s, t in outs],
        in_specs=[pl.BlockSpec(memory_space=space)] * len(args),
        out_specs=[pl.BlockSpec(memory_space=pltpu.VMEM)] * len(outs),
        scratch_shapes=scratch,
        compiler_params=pltpu.CompilerParams(vmem_limit_bytes=VMEM),
    )(*args)


def exchange(sz, msg, rows):
    blocks = msg.reshape(sz.devices, 1, rows * sz.cams)
    got = lax.all_to_all(blocks, "rows", split_axis=0, concat_axis=0, tiled=True)
    return got.reshape(sz.devices * rows, sz.cams)


def local(right_side, diag_blocks, precond, upper_blocks, block_cols, slot_of_camera):
    block, cams = right_side.shape
    lists = block_cols.shape[0]
    sz = Sizes(block, lists, cams, lax.axis_size("rows"))
    field = ((block, cams), F32)
    index = ((lists, cams), I32)
    hot_type = ((sz.entries, cams), BF16)
    upper_blocks = upper_blocks.transpose(1, 2, 0, 3)
    table = slot_of_camera.reshape(-1, cams)
    tall = pltpu.VMEM((lists * TALL, cams), F32)

    def turns(pk):
        return pltpu.VMEM((pk.rows, pk.groups, sz.devices, cams), F32)

    ins = (block_cols, table, right_side, precond, upper_blocks, diag_blocks)
    msg, own, off, chunk, z, lane, right_side, precond, upper_blocks, diag_blocks = call(
        functools.partial(first_kernel, sz), "first",
        [((sz.devices * sz.one.stride, cams), F32), index, index, index, field, hot_type]
        + [(x.shape, x.dtype) for x in ins[2:]],
        [pltpu.VMEM(x.shape, x.dtype) for x in ins[:2]]
        + [tall, tall, pltpu.SemaphoreType.DMA((len(ins),))],
        *(pltpu.with_memory_space_constraint(x, pltpu.HBM) for x in ins), space=pltpu.HBM,
    )
    got = exchange(sz, msg, sz.one.stride)
    msg, q, w, hot = call(
        functools.partial(second_kernel, sz), "second",
        [((sz.devices * sz.two.stride, cams), F32), field, field, hot_type],
        [tall] * 4 + [turns(sz.one)],
        got, right_side, z, own, off, chunk, lane, diag_blocks, precond, upper_blocks,
    )
    got = exchange(sz, msg, sz.two.stride)
    part, new_dot, sol, res, direction, image = call(
        functools.partial(third_kernel, sz), "third",
        [((sz.devices, cams), F32), ((1, cams), F32)] + [field] * 4,
        [tall] * 3 + [turns(sz.two)],
        got, right_side, z, q, w, chunk, lane, hot, diag_blocks, upper_blocks,
    )
    parts = exchange(sz, part, 1)
    return tuple(
        call(
            fourth_kernel, "fourth", [field, field], [],
            parts, new_dot, sol, res, direction, image,
        )
    )


def solution(mesh):
    return jax.shard_map(
        local,
        mesh=mesh,
        in_specs=(
            P(None, "rows"),
            P(None, None, "rows"),
            P(None, None, "rows"),
            P(None, None, None, "rows"),
            P(None, "rows"),
            P(),
        ),
        out_specs=(P(None, "rows"), P(None, "rows")),
        check_vma=False,
    )
```

time: 42.8 us -> 40.8 us (0.953)
  Pallas kernels: 7.02 us -> 4.97 us
    pallas_call x4, Pallas kernels: 7.02 us -> 4.97 us  [call(): pl.pallas_call(body, name=name, out_shape=[jax.ShapeDtypeStruct(s, t) for...]
where the time goes in v3:
time: 40.8 us; the launch traced here: 40.6 us
  blocking collectives  34.9 us (86%)
  Pallas kernels  4.97 us (12%)
  between operations  0.65 us (2%)
    all_to_all x3, blocking collectives, exchange(): lax.all_to_all(blocks, 'rows', split_axis=0, concat_axis=0, tiled=True)  34.9 us
    pallas_call x4, Pallas kernels, call(): pl.pallas_call(body, name=name, out_shape=[jax.ShapeDtypeStruct(s, t) for...  4.97 us

profile of v3, /device:TPU:0, one launch (start us, length us, event | category | flops | bytes accessed | tf_op | source)
XLA Modules:
  0.0 40.6 jit_solution(5737176329691306443)
XLA Ops:
  0.6 1.9 %first.1 = (f32[384,128]{1,0:T(8,128)S(1)}, s32[8,128]{1,0:T(8,128)S(1)}, s32[8,128]{1,0:T(8,128)S(1)}, s32[8,128]{1,0:T(8,128)S(1)}, f32[9,128]{1,0:T(8,128)S(1...) custom-call(s32[8,128]{1,0:T(8,128)} %cols_hbm.1, ...), custom_call_target="tpu_custom_call" | custom-call | tf_op jit(solution)/shard_map/first/pallas_call | solution.py:361
  2.5 16.1 %all_to_all.15 = f32[32,1,1536]{2,1,0:T(1,128)S(1)} all-to-all(f32[32,1,1536]{2,1,0:T(1,128)S(1)} %bitcast.12), channel_id=1, replica_groups=mesh['rows'=32] {'rows'}, dimensions={0} | all-to-all | bytes 393216 | tf_op jit(solution)/shard_map/all_to_all | solution.py:374
  18.6 1.9 %second.1 = (f32[160,128]{1,0:T(8,128)S(1)}, f32[9,128]{1,0:T(8,128)S(1)}, f32[9,128]{1,0:T(8,128)S(1)}, bf16[1024,128]{1,0:T(8,128)(2,1)S(1)}) custom-call(f32[384,128]{1,0:T(8,128)S(1)} %bitcast.10, f32[9,128]{1,0:T(8,128)S(1)} %get-tuple-element.23.rhs_ref, f32[9,128]{1,0:T(8,128)S(1)} %get-tuple-element.24.z_ref, ...), custom_call_target="tpu_custom_call" | custom-call | tf_op jit(solution)/shard_map/second/pallas_call | solution.py:361
  20.5 10.0 %all_to_all.16 = f32[32,1,640]{2,1,0:T(1,128)S(1)} all-to-all(f32[32,1,640]{2,1,0:T(1,128)S(1)} %bitcast.13), channel_id=1, replica_groups=mesh['rows'=32] {'rows'}, dimensions={0} | all-to-all | bytes 163840 | tf_op jit(solution)/shard_map/all_to_all | solution.py:374
  30.5 0.6 %third.1 = (f32[32,128]{1,0:T(8,128)S(1)}, f32[1,128]{1,0:T(1,128)S(1)}, f32[9,128]{1,0:T(8,128)S(1)}, f32[9,128]{1,0:T(8,128)S(1)}, f32[9,128]{1,0:T(8,128)S(1)}, /*index=5*/f32[9,128]{1,0:T(8,128)S(1)}) custom-call(f32[160,128]{1,0:T(8,128)S(1)} %bitcast.11, f32[9,128]{1,0:T(8,128)S(1)} %get-tuple-element.23.rhs_ref, ...), custom_call_target="tpu_custom_call" | custom-call | tf_op jit(solution)/shard_map/third/pallas_call | solution.py:361
  31.1 8.9 %all_to_all.17 = f32[32,1,128]{2,1,0:T(1,128)S(1)} all-to-all(f32[32,1,128]{2,1,0:T(1,128)S(1)} %bitcast.15), channel_id=1, replica_groups=mesh['rows'=32] {'rows'}, dimensions={0} | all-to-all | bytes 32768 | tf_op jit(solution)/shard_map/all_to_all | solution.py:374
  39.9 0.6 %fourth.1 = (f32[9,128]{1,0:T(8,128)}, f32[9,128]{1,0:T(8,128)}) custom-call(f32[32,128]{1,0:T(8,128)S(1)} %bitcast.14, f32[1,128]{1,0:T(1,128)S(1)} %get-tuple-element.37.dot_ref, f32[9,128]{1,0:T(8,128)S(1)} %get-tuple-element.38.sol_ref, f32[9,128]{1,0:T(8,128)S(1)} %get-tuple-element.39.res_ref, f32[9,128]{1,0:T(8,128)S(1)} %get-tuple-element.40.dir_ref, ...), custom_call_target="tpu_custom_call" | custom-call | tf_op jit(solution)/shard_map/fourth/pallas_call | solution.py:361

commit v4 on v3

--- a/solution.py
+++ b/solution.py
@@ -62,12 +62,35 @@
 
 
 def stacked(x):
-    return jnp.concatenate(split3(x), axis=0)
+    parts = [p.astype(F32) for p in split3(x)]
+    row = lax.broadcasted_iota(I32, (8, x.shape[1]), 0)
+    tail = parts[0][8:]
+    for at in (1, 2):
+        tail = jnp.where(row < 2 * at, tail, pltpu.roll(parts[at][8:], 2 * at, 0))
+    return jnp.concatenate([p[:8] for p in parts] + [tail], axis=0).astype(BF16)
 
 
 def folded(x):
-    height = x.shape[0] // 3
-    return x[:height] + x[height : 2 * height] + x[2 * height :]
+    tail = x[24:]
+    tail = tail + pltpu.roll(tail, 6, 0) + pltpu.roll(tail, 4, 0)
+    return jnp.concatenate([x[:8] + x[8:16] + x[16:24], tail], axis=0)
+
+
+def row_sums(arrays):
+    shape = arrays[0].shape
+    if len(arrays) != 8 or shape[0] != 8:
+        return jnp.concatenate([col_sum(x) for x in arrays], axis=0)
+    row = lax.broadcasted_iota(I32, shape, 0)
+    step = 4
+    while step:
+        low = (row & step) == 0
+        arrays = [
+            jnp.where(low, a, b)
+            + jnp.where(low, pltpu.roll(a, 8 - step, 0), pltpu.roll(b, step, 0))
+            for a, b in zip(arrays[: len(arrays) // 2], arrays[len(arrays) // 2 :])
+        ]
+        step //= 2
+    return arrays[0]
 
 
 def dot(a, b):
@@ -101,18 +124,20 @@
 
 
 def block_apply(sz, blocks_ref, v):
-    return jnp.concatenate([col_sum(blocks_ref[a] * v) for a in range(sz.block)], axis=0)
-
-
-def upper_apply(sz, up_ref, col_ref):
-    gathered = [col_ref[pl.ds(b, sz.lists, stride=TALL), :] for b in range(sz.block)]
+    acc = blocks_ref[0] * v[0:1]
+    for b in range(1, sz.block):
+        acc = acc + blocks_ref[b] * v[b : b + 1]
+    return acc
+
+
+def upper_apply(sz, up_ref, gathered):
     rows = []
     for a in range(sz.block):
         acc = up_ref[a, 0] * gathered[0]
         for b in range(1, sz.block):
             acc = acc + up_ref[a, b] * gathered[b]
-        rows.append(col_sum(acc))
-    return jnp.concatenate(rows, axis=0)
+        rows.append(acc)
+    return jnp.concatenate([row_sums(rows[:8])] + [col_sum(x) for x in rows[8:]], axis=0)
 
 
 def side_by_side(ref, height):
@@ -136,7 +161,8 @@
         for at in range(sz.lists)
     ]
     res = dot_t(jnp.concatenate(left, axis=0), side_by_side(lane_ref, sz.cams))
-    return [folded(res[at * 3 * TALL : (at + 1) * 3 * TALL]) for at in range(sz.lists)]
+    height = parts.shape[0]
+    return [folded(res[at * height : (at + 1) * height]) for at in range(sz.lists)]
 
 
 def pack(sz, pk, value_of, msg_ref):
@@ -180,30 +206,34 @@
     return folded(dot_t(parts, side_by_side(hot_ref, sz.cams)))[: sz.block]
 
 
-def gather(sz, msg_ref, own, off, col_ref):
-    c = sz.cams
-    rows = sz.one.stride
-    left = jnp.concatenate(split3(msg_ref[...]), axis=1)
-    period = math.lcm(rows, 8)
-    per = period // rows
-    width = 2 * c
-    row = iota((period, width), 0)
-    owner_at = jnp.zeros((period, width), I32)
-    for q in range(1, per):
-        owner_at = owner_at + jnp.where(row >= q * rows, 1, 0)
+def gather(sz, msg_ref, own, off):
+    c, stride = sz.cams, sz.one.stride
+    high = sz.devices // 4
+    left = []
+    for low in range(4):
+        rows = []
+        for b in range(sz.block):
+            x = msg_ref[pl.ds(low * stride + b, high, stride=4 * stride), :]
+            rows += [p.astype(F32) for p in split3(x)]
+        left.append(jnp.concatenate(rows, axis=0))
+    left = jnp.concatenate(left, axis=1).astype(BF16)
+    out = [[] for _ in range(sz.block)]
+    zeros = jnp.zeros((c, 2 * c), BF16)
     for k in range(0, sz.lists, 2):
         pair = jnp.concatenate([off[k : k + 1], off[k + 1 : k + 2]], axis=1)
-        right = hot_rows(pair, (c, width))
-        res = dot(left, jnp.concatenate([right] * 3, axis=0))
-        owner = jnp.concatenate([own[k : k + 1], own[k + 1 : k + 2]], axis=1) - owner_at
-        acc = jnp.zeros((period, width), F32)
-        for m in range(sz.devices // per):
-            acc = jnp.where(owner == m * per, res[m * period : (m + 1) * period], acc)
-        g = acc[: sz.block]
-        for q in range(1, per):
-            g = g + acc[q * rows : q * rows + sz.block]
-        col_ref[pl.ds(k * TALL, sz.block), :] = g[:, :c]
-        col_ref[pl.ds((k + 1) * TALL, sz.block), :] = g[:, c:]
+        owner = jnp.concatenate([own[k : k + 1], own[k + 1 : k + 2]], axis=1)
+        hot = hot_rows(pair, (c, 2 * c))
+        low = jnp.broadcast_to((owner & 3).astype(F32).astype(BF16), hot.shape)
+        right = [jnp.where(low == jnp.full(hot.shape, at, BF16), hot, zeros) for at in range(4)]
+        res = dot(left, jnp.concatenate(right, axis=0))
+        here = iota((high, 2 * c), 0) == (owner >> 2)
+        for b in range(sz.block):
+            at = 3 * high * b
+            x = res[at : at + high] + res[at + high : at + 2 * high] + res[at + 2 * high :][:high]
+            x = jnp.where(here, x, 0.0)
+            x = sum(x[i : i + 8] for i in range(0, high, 8))
+            out[b] += [x[:, :c], x[:, c:]]
+    return [row_sums(x) for x in out]
 
 
 def to_lists(sz, values, chunk, lane_ref, tall_ref, col_ref):
@@ -218,6 +248,7 @@
         for at in range(1, sz.lists):
             out = jnp.where(chunk[k : k + 1] == at, res[at * TALL : (at + 1) * TALL, lanes], out)
         col_ref[k * TALL : (k + 1) * TALL, :] = out
+    return [col_ref[pl.ds(b, sz.lists, stride=TALL), :] for b in range(sz.block)]
 
 
 def first_kernel(
@@ -232,9 +263,15 @@
     copies = [pltpu.make_async_copy(a, b, sems.at[i]) for i, (a, b) in enumerate(pairs)]
     for copy in copies:
         copy.start()
-    copies[0].wait()
-    copies[1].wait()
+    for copy in copies[:4]:
+        copy.wait()
     c = sz.cams
+    pk = sz.one
+    z = block_apply(sz, pre_ref, rhs_ref[...])
+    z_ref[...] = z
+    for b in range(sz.block):
+        at = pl.ds(b, sz.devices, stride=pk.stride)
+        msg_ref[at, :] = jnp.broadcast_to(z[b : b + 1], (sz.devices, c))
     cols = cols_ref[...]
     table = table_ref[...]
     height = table.shape[0]
@@ -271,14 +308,8 @@
     for k in range(sz.lists):
         lane_ref[k * c : (k + 1) * c, :] = hot_rows(place[k : k + 1], (c, c))
 
-    for copy in copies[2:]:
+    for copy in copies[4:]:
         copy.wait()
-    pk = sz.one
-    z = block_apply(sz, pre_ref, rhs_ref[...])
-    z_ref[...] = z
-    for b in range(sz.block):
-        at = pl.ds(b, sz.devices, stride=pk.stride)
-        msg_ref[at, :] = jnp.broadcast_to(z[b : b + 1], (sz.devices, c))
     for at, x in enumerate(bucketed(sz, z, off, up_ref, chunk, lane_ref, val_ref)):
         tall_ref[at * TALL : (at + 1) * TALL, :] = x
     pack(sz, pk, lambda v: tall_ref[pl.ds(v, sz.lists, stride=TALL), :], msg_ref)
@@ -287,7 +318,7 @@
 def second_kernel(
     sz, got_ref, rhs_ref, z_ref, own_ref, off_ref, chunk_ref, lane_ref, diag_ref, pre_ref, up_ref,
     msg_ref, q_ref, w_ref, hot_ref,
-    val_ref, tall_ref, ans_ref, col_ref, turn_ref,
+    val_ref, tall_ref, ans_ref, turn_ref,
 ):
     c = sz.cams
     b, z = rhs_ref[...], z_ref[...]
@@ -296,8 +327,8 @@
     for at in range(sz.lists):
         hot_ref[at * c : (at + 1) * c, :] = hot_rows(wanted[at : at + 1], (c, c))
     pushed = scatter(sz, values, val_ref, hot_ref)
-    gather(sz, got_ref, own_ref[...], off_ref[...], col_ref)
-    q = block_apply(sz, diag_ref, z) + upper_apply(sz, up_ref, col_ref) + pushed
+    gathered = gather(sz, got_ref, own_ref[...], off_ref[...])
+    q = block_apply(sz, diag_ref, z) + upper_apply(sz, up_ref, gathered) + pushed
     w = block_apply(sz, pre_ref, q)
     q_ref[...] = q
     w_ref[...] = w
@@ -330,9 +361,11 @@
 ):
     b, z, q, w = rhs_ref[...], z_ref[...], q_ref[...], w_ref[...]
     values = unpack(sz, sz.two, got_ref, turn_ref)
-    to_lists(sz, values[sz.answer :], chunk_ref[...], lane_ref, tall_ref, col_ref)
+    gathered = to_lists(
+        sz, values[sz.answer :], chunk_ref[...], lane_ref, tall_ref, col_ref
+    )
     pushed = scatter(sz, values, val_ref, hot_ref)
-    y = block_apply(sz, diag_ref, w) + upper_apply(sz, up_ref, col_ref) + pushed
+    y = block_apply(sz, diag_ref, w) + upper_apply(sz, up_ref, gathered) + pushed
     sums = col_sum(values[sz.block])
     lane = iota(sums.shape, 1) & (sz.refs - 1)
     bz, zq, bw, qw = [
@@ -402,7 +435,7 @@
     msg, q, w, hot = call(
         functools.partial(second_kernel, sz), "second",
         [((sz.devices * sz.two.stride, cams), F32), field, field, hot_type],
-        [tall] * 4 + [turns(sz.one)],
+        [tall] * 3 + [turns(sz.one)],
         got, right_side, z, own, off, chunk, lane, diag_blocks, precond, upper_blocks,
     )
     got = exchange(sz, msg, sz.two.stride)

time: 40.8 us -> 40 us (0.980)
  Pallas kernels: 4.97 us -> 4.22 us
    pallas_call x4, Pallas kernels: 4.97 us -> 4.22 us  [call(): pl.pallas_call(body, name=name, out_shape=[jax.ShapeDtypeStruct(s, t) for...]
where the time goes in v4:
time: 40 us; the launch traced here: 39.8 us
  blocking collectives  34.9 us (87%)
  Pallas kernels  4.22 us (11%)
  between operations  0.65 us (2%)
    all_to_all x3, blocking collectives, exchange(): lax.all_to_all(blocks, 'rows', split_axis=0, concat_axis=0, tiled=True)  34.9 us
    pallas_call x4, Pallas kernels, call(): pl.pallas_call(body, name=name, out_shape=[jax.ShapeDtypeStruct(s, t) for...  4.22 us

profile of v4, /device:TPU:0, one launch (start us, length us, event | category | flops | bytes accessed | tf_op | source)
XLA Modules:
  0.0 39.8 jit_solution(16899461042358245649)
XLA Ops:
  0.6 1.8 %first.1 = (f32[384,128]{1,0:T(8,128)S(1)}, s32[8,128]{1,0:T(8,128)S(1)}, s32[8,128]{1,0:T(8,128)S(1)}, s32[8,128]{1,0:T(8,128)S(1)}, f32[9,128]{1,0:T(8,128)S(1...) custom-call(s32[8,128]{1,0:T(8,128)} %cols_hbm.1, ...), custom_call_target="tpu_custom_call" | custom-call | tf_op jit(solution)/shard_map/first/pallas_call | solution.py:394
  2.5 16.1 %all_to_all.15 = f32[32,1,1536]{2,1,0:T(1,128)S(1)} all-to-all(f32[32,1,1536]{2,1,0:T(1,128)S(1)} %bitcast.12), channel_id=1, replica_groups=mesh['rows'=32] {'rows'}, dimensions={0} | all-to-all | bytes 393216 | tf_op jit(solution)/shard_map/all_to_all | solution.py:407
  18.5 1.2 %second.1 = (f32[160,128]{1,0:T(8,128)S(1)}, f32[9,128]{1,0:T(8,128)S(1)}, f32[9,128]{1,0:T(8,128)S(1)}, bf16[1024,128]{1,0:T(8,128)(2,1)S(1)}) custom-call(f32[384,128]{1,0:T(8,128)S(1)} %bitcast.10, f32[9,128]{1,0:T(8,128)S(1)} %get-tuple-element.23.rhs_ref, f32[9,128]{1,0:T(8,128)S(1)} %get-tuple-element.24.z_ref, ...), custom_call_target="tpu_custom_call" | custom-call | tf_op jit(solution)/shard_map/second/pallas_call | solution.py:394
  19.7 10.0 %all_to_all.16 = f32[32,1,640]{2,1,0:T(1,128)S(1)} all-to-all(f32[32,1,640]{2,1,0:T(1,128)S(1)} %bitcast.13), channel_id=1, replica_groups=mesh['rows'=32] {'rows'}, dimensions={0} | all-to-all | bytes 163840 | tf_op jit(solution)/shard_map/all_to_all | solution.py:407
  29.7 0.6 %third.1 = (f32[32,128]{1,0:T(8,128)S(1)}, f32[1,128]{1,0:T(1,128)S(1)}, f32[9,128]{1,0:T(8,128)S(1)}, f32[9,128]{1,0:T(8,128)S(1)}, f32[9,128]{1,0:T(8,128)S(1)}, /*index=5*/f32[9,128]{1,0:T(8,128)S(1)}) custom-call(f32[160,128]{1,0:T(8,128)S(1)} %bitcast.11, f32[9,128]{1,0:T(8,128)S(1)} %get-tuple-element.23.rhs_ref, ...), custom_call_target="tpu_custom_call" | custom-call | tf_op jit(solution)/shard_map/third/pallas_call | solution.py:394
  30.3 8.9 %all_to_all.17 = f32[32,1,128]{2,1,0:T(1,128)S(1)} all-to-all(f32[32,1,128]{2,1,0:T(1,128)S(1)} %bitcast.15), channel_id=1, replica_groups=mesh['rows'=32] {'rows'}, dimensions={0} | all-to-all | bytes 32768 | tf_op jit(solution)/shard_map/all_to_all | solution.py:407
  39.2 0.6 %fourth.1 = (f32[9,128]{1,0:T(8,128)}, f32[9,128]{1,0:T(8,128)}) custom-call(f32[32,128]{1,0:T(8,128)S(1)} %bitcast.14, f32[1,128]{1,0:T(1,128)S(1)} %get-tuple-element.37.dot_ref, f32[9,128]{1,0:T(8,128)S(1)} %get-tuple-element.38.sol_ref, f32[9,128]{1,0:T(8,128)S(1)} %get-tuple-element.39.res_ref, f32[9,128]{1,0:T(8,128)S(1)} %get-tuple-element.40.dir_ref, ...), custom_call_target="tpu_custom_call" | custom-call | tf_op jit(solution)/shard_map/fourth/pallas_call | solution.py:394

commit v5 on v4

--- a/solution.py
+++ b/solution.py
@@ -332,7 +332,7 @@
     w = block_apply(sz, pre_ref, q)
     q_ref[...] = q
     w_ref[...] = w
-    dots = [total(b * z), total(z * q), total(b * w), total(q * w)]
+    dots = [total(b * z), total(z * q)]
     lane = iota((sz.lists, c), 1) & (sz.refs - 1)
     dot_rows = jnp.zeros((sz.lists, c), F32)
     for at, d in enumerate(dots):
@@ -356,38 +356,52 @@
 
 def third_kernel(
     sz, got_ref, rhs_ref, z_ref, q_ref, w_ref, chunk_ref, lane_ref, hot_ref, diag_ref, up_ref,
-    part_ref, dot_ref, sol_ref, res_ref, dir_ref, img_ref,
+    part_ref, known_ref, res_ref, pre_ref, img_ref,
     val_ref, tall_ref, col_ref, turn_ref,
 ):
     b, z, q, w = rhs_ref[...], z_ref[...], q_ref[...], w_ref[...]
     values = unpack(sz, sz.two, got_ref, turn_ref)
+    sums = col_sum(values[sz.block])
+    lane = iota(sums.shape, 1) & (sz.refs - 1)
+    res_dot, curve = [
+        jnp.sum(jnp.where(lane == at, sums, 0.0), axis=1, keepdims=True) for at in range(2)
+    ]
+    step = res_dot / curve
     gathered = to_lists(
         sz, values[sz.answer :], chunk_ref[...], lane_ref, tall_ref, col_ref
     )
     pushed = scatter(sz, values, val_ref, hot_ref)
     y = block_apply(sz, diag_ref, w) + upper_apply(sz, up_ref, gathered) + pushed
-    sums = col_sum(values[sz.block])
-    lane = iota(sums.shape, 1) & (sz.refs - 1)
-    bz, zq, bw, qw = [
-        jnp.sum(jnp.where(lane == at, sums, 0.0), axis=1, keepdims=True) for at in range(4)
+    residual = b - step * q
+    pre = z - step * w
+    image = q - step * y
+    res_ref[...] = residual
+    pre_ref[...] = pre
+    img_ref[...] = image
+    known = [res_dot, curve, step]
+    known_ref[...] = jnp.concatenate([jnp.broadcast_to(x, (1, sz.cams)) for x in known], axis=0)
+    dots = [total(residual * pre), total(pre * image), total(pre * q + z * image)]
+    row = dots[2]
+    lane = iota((1, sz.cams), 1) & 3
+    for at in (1, 0):
+        row = jnp.where(lane == at, dots[at], row)
+    part_ref[...] = jnp.broadcast_to(row, part_ref.shape)
+
+
+def fourth_kernel(
+    part_ref, known_ref, z_ref, q_ref, res_ref, pre_ref, img_ref, out_ref, left_ref
+):
+    sums = col_sum(part_ref[...])
+    lane = iota(sums.shape, 1)
+    new_dot, pre_curve, cross = [
+        jnp.sum(jnp.where(lane == at, sums, 0.0), axis=1, keepdims=True) for at in range(3)
     ]
-    step = bz / zq
-    new_dot = bz - step * (zq + bw) + step * step * qw
-    beta = new_dot / bz
-    direction = (1.0 + beta) * z - step * w
-    image = (1.0 + beta) * q - step * y
-    sol_ref[...] = step * z
-    res_ref[...] = b - step * q
-    dir_ref[...] = direction
-    img_ref[...] = image
-    dot_ref[...] = jnp.broadcast_to(new_dot, dot_ref.shape)
-    part_ref[...] = jnp.broadcast_to(total(direction * image), part_ref.shape)
-
-
-def fourth_kernel(part_ref, dot_ref, sol_ref, res_ref, dir_ref, img_ref, out_ref, left_ref):
-    step = dot_ref[...] / col_sum(part_ref[...])
-    out_ref[...] = sol_ref[...] + step * dir_ref[...]
-    left_ref[...] = res_ref[...] - step * img_ref[...]
+    res_dot, curve, step = known_ref[0:1], known_ref[1:2], known_ref[2:3]
+    z = z_ref[...]
+    beta = new_dot / res_dot
+    next_step = new_dot / (pre_curve + beta * (cross + beta * curve))
+    out_ref[...] = step * z + next_step * (pre_ref[...] + beta * z)
+    left_ref[...] = res_ref[...] - next_step * (img_ref[...] + beta * q_ref[...])
 
 
 def call(body, name, outs, scratch, *args, space=pltpu.VMEM):
@@ -439,9 +453,9 @@
         got, right_side, z, own, off, chunk, lane, diag_blocks, precond, upper_blocks,
     )
     got = exchange(sz, msg, sz.two.stride)
-    part, new_dot, sol, res, direction, image = call(
+    part, known, res, pre, image = call(
         functools.partial(third_kernel, sz), "third",
-        [((sz.devices, cams), F32), ((1, cams), F32)] + [field] * 4,
+        [((sz.devices, cams), F32), ((3, cams), F32)] + [field] * 3,
         [tall] * 3 + [turns(sz.two)],
         got, right_side, z, q, w, chunk, lane, hot, diag_blocks, upper_blocks,
     )
@@ -449,7 +463,7 @@
     return tuple(
         call(
             fourth_kernel, "fourth", [field, field], [],
-            parts, new_dot, sol, res, direction, image,
+            parts, known, z, q, res, pre, image,
         )
     )
 

time: 40 us -> 40.1 us (level)
  no operation moved by 1% of the time
where the time goes in v5:
time: 40.1 us; the launch traced here: 39.9 us
  blocking collectives  34.9 us (87%)
  Pallas kernels  4.31 us (11%)
  between operations  0.65 us (2%)
    all_to_all x3, blocking collectives, exchange(): lax.all_to_all(blocks, 'rows', split_axis=0, concat_axis=0, tiled=True)  34.9 us
    pallas_call x4, Pallas kernels, call(): pl.pallas_call(body, name=name, out_shape=[jax.ShapeDtypeStruct(s, t) for...  4.31 us

profile of v5, /device:TPU:0, one launch (start us, length us, event | category | flops | bytes accessed | tf_op | source)
XLA Modules:
  0.0 39.9 jit_solution(10659228308085285970)
XLA Ops:
  0.6 1.8 %first.1 = (f32[384,128]{1,0:T(8,128)S(1)}, s32[8,128]{1,0:T(8,128)S(1)}, s32[8,128]{1,0:T(8,128)S(1)}, s32[8,128]{1,0:T(8,128)S(1)}, f32[9,128]{1,0:T(8,128)S(1...) custom-call(s32[8,128]{1,0:T(8,128)} %cols_hbm.1, ...), custom_call_target="tpu_custom_call" | custom-call | tf_op jit(solution)/shard_map/first/pallas_call | solution.py:408
  2.4 16.1 %all_to_all.15 = f32[32,1,1536]{2,1,0:T(1,128)S(1)} all-to-all(f32[32,1,1536]{2,1,0:T(1,128)S(1)} %bitcast.12), channel_id=1, replica_groups=mesh['rows'=32] {'rows'}, dimensions={0} | all-to-all | bytes 393216 | tf_op jit(solution)/shard_map/all_to_all | solution.py:421
  18.5 1.2 %second.1 = (f32[160,128]{1,0:T(8,128)S(1)}, f32[9,128]{1,0:T(8,128)S(1)}, f32[9,128]{1,0:T(8,128)S(1)}, bf16[1024,128]{1,0:T(8,128)(2,1)S(1)}) custom-call(f32[384,128]{1,0:T(8,128)S(1)} %bitcast.10, f32[9,128]{1,0:T(8,128)S(1)} %get-tuple-element.22.rhs_ref, f32[9,128]{1,0:T(8,128)S(1)} %get-tuple-element.23.z_ref, ...), custom_call_target="tpu_custom_call" | custom-call | tf_op jit(solution)/shard_map/second/pallas_call | solution.py:408
  19.7 10.0 %all_to_all.16 = f32[32,1,640]{2,1,0:T(1,128)S(1)} all-to-all(f32[32,1,640]{2,1,0:T(1,128)S(1)} %bitcast.13), channel_id=1, replica_groups=mesh['rows'=32] {'rows'}, dimensions={0} | all-to-all | bytes 163840 | tf_op jit(solution)/shard_map/all_to_all | solution.py:421
  29.7 0.6 %third.1 = (f32[32,128]{1,0:T(8,128)S(1)}, f32[3,128]{1,0:T(4,128)S(1)}, f32[9,128]{1,0:T(8,128)S(1)}, f32[9,128]{1,0:T(8,128)S(1)}, f32[9,128]{1,0:T(8,128)S(1)}) custom-call(f32[160,128]{1,0:T(8,128)S(1)} %bitcast.11, f32[9,128]{1,0:T(8,128)S(1)} %get-tuple-element.22.rhs_ref, f32[9,128]{1,0:T(8,128)S(1)} %get-tuple-element.23.z_ref, ...), custom_call_target="tpu_custom_call" | custom-call | tf_op jit(solution)/shard_map/third/pallas_call | solution.py:408
  30.3 8.9 %all_to_all.17 = f32[32,1,128]{2,1,0:T(1,128)S(1)} all-to-all(f32[32,1,128]{2,1,0:T(1,128)S(1)} %bitcast.15), channel_id=1, replica_groups=mesh['rows'=32] {'rows'}, dimensions={0} | all-to-all | bytes 32768 | tf_op jit(solution)/shard_map/all_to_all | solution.py:421
  39.2 0.7 %fourth.1 = (f32[9,128]{1,0:T(8,128)}, f32[9,128]{1,0:T(8,128)}) custom-call(f32[32,128]{1,0:T(8,128)S(1)} %bitcast.14, f32[3,128]{1,0:T(4,128)S(1)} %get-tuple-element.36.known_ref, f32[9,128]{1,0:T(8,128)S(1)} %get-tuple-element.23.z_ref, f32[9,128]{1,0:T(8,128)S(1)} %get-tuple-element.32.q_ref, f32[9,128]{1,0:T(8,128)S(1)} %get-tuple-element.37.res_ref, ...), custom_call_target="tpu_custom_call" | custom-call | tf_op jit(solution)/shard_map/fourth/pallas_call | solution.py:408

commit v6 on v5

--- a/solution.py
+++ b/solution.py
@@ -317,7 +317,7 @@
 
 def second_kernel(
     sz, got_ref, rhs_ref, z_ref, own_ref, off_ref, chunk_ref, lane_ref, diag_ref, pre_ref, up_ref,
-    msg_ref, q_ref, w_ref, hot_ref,
+    msg_ref, q_ref, side_ref, hot_ref,
     val_ref, tall_ref, ans_ref, turn_ref,
 ):
     c = sz.cams
@@ -328,10 +328,11 @@
         hot_ref[at * c : (at + 1) * c, :] = hot_rows(wanted[at : at + 1], (c, c))
     pushed = scatter(sz, values, val_ref, hot_ref)
     gathered = gather(sz, got_ref, own_ref[...], off_ref[...])
-    q = block_apply(sz, diag_ref, z) + upper_apply(sz, up_ref, gathered) + pushed
+    side = upper_apply(sz, up_ref, gathered) + pushed
+    q = block_apply(sz, diag_ref, z) + side
     w = block_apply(sz, pre_ref, q)
     q_ref[...] = q
-    w_ref[...] = w
+    side_ref[...] = side
     dots = [total(b * z), total(z * q)]
     lane = iota((sz.lists, c), 1) & (sz.refs - 1)
     dot_rows = jnp.zeros((sz.lists, c), F32)
@@ -355,11 +356,12 @@
 
 
 def third_kernel(
-    sz, got_ref, rhs_ref, z_ref, q_ref, w_ref, chunk_ref, lane_ref, hot_ref, diag_ref, up_ref,
-    part_ref, known_ref, res_ref, pre_ref, img_ref,
+    sz, got_ref, rhs_ref, z_ref, q_ref, side_ref, chunk_ref, lane_ref, hot_ref,
+    diag_ref, pre_ref, up_ref,
+    part_ref, known_ref, res_ref, dir_ref, img_ref,
     val_ref, tall_ref, col_ref, turn_ref,
 ):
-    b, z, q, w = rhs_ref[...], z_ref[...], q_ref[...], w_ref[...]
+    b, z, q = rhs_ref[...], z_ref[...], q_ref[...]
     values = unpack(sz, sz.two, got_ref, turn_ref)
     sums = col_sum(values[sz.block])
     lane = iota(sums.shape, 1) & (sz.refs - 1)
@@ -367,16 +369,16 @@
         jnp.sum(jnp.where(lane == at, sums, 0.0), axis=1, keepdims=True) for at in range(2)
     ]
     step = res_dot / curve
+    residual = b - step * q
+    pre = block_apply(sz, pre_ref, residual)
     gathered = to_lists(
         sz, values[sz.answer :], chunk_ref[...], lane_ref, tall_ref, col_ref
     )
     pushed = scatter(sz, values, val_ref, hot_ref)
-    y = block_apply(sz, diag_ref, w) + upper_apply(sz, up_ref, gathered) + pushed
-    residual = b - step * q
-    pre = z - step * w
-    image = q - step * y
+    side = side_ref[...] - step * (upper_apply(sz, up_ref, gathered) + pushed)
+    image = block_apply(sz, diag_ref, pre) + side
     res_ref[...] = residual
-    pre_ref[...] = pre
+    dir_ref[...] = pre
     img_ref[...] = image
     known = [res_dot, curve, step]
     known_ref[...] = jnp.concatenate([jnp.broadcast_to(x, (1, sz.cams)) for x in known], axis=0)
@@ -446,7 +448,7 @@
         *(pltpu.with_memory_space_constraint(x, pltpu.HBM) for x in ins), space=pltpu.HBM,
     )
     got = exchange(sz, msg, sz.one.stride)
-    msg, q, w, hot = call(
+    msg, q, side, hot = call(
         functools.partial(second_kernel, sz), "second",
         [((sz.devices * sz.two.stride, cams), F32), field, field, hot_type],
         [tall] * 3 + [turns(sz.one)],
@@ -457,7 +459,7 @@
         functools.partial(third_kernel, sz), "third",
         [((sz.devices, cams), F32), ((3, cams), F32)] + [field] * 3,
         [tall] * 3 + [turns(sz.two)],
-        got, right_side, z, q, w, chunk, lane, hot, diag_blocks, upper_blocks,
+        got, right_side, z, q, side, chunk, lane, hot, diag_blocks, precond, upper_blocks,
     )
     parts = exchange(sz, part, 1)
     return tuple(

time: 40.1 us -> 40.1 us (level)
  no operation moved by 1% of the time
where the time goes in v6:
time: 40.1 us; the launch traced here: 39.9 us
  blocking collectives  34.9 us (87%)
  Pallas kernels  4.3 us (11%)
  between operations  0.65 us (2%)
    all_to_all x3, blocking collectives, exchange(): lax.all_to_all(blocks, 'rows', split_axis=0, concat_axis=0, tiled=True)  34.9 us
    pallas_call x4, Pallas kernels, call(): pl.pallas_call(body, name=name, out_shape=[jax.ShapeDtypeStruct(s, t) for...  4.3 us

profile of v6, /device:TPU:0, one launch (start us, length us, event | category | flops | bytes accessed | tf_op | source)
XLA Modules:
  0.0 39.9 jit_solution(11225903938823337607)
XLA Ops:
  0.6 1.8 %first.1 = (f32[384,128]{1,0:T(8,128)S(1)}, s32[8,128]{1,0:T(8,128)S(1)}, s32[8,128]{1,0:T(8,128)S(1)}, s32[8,128]{1,0:T(8,128)S(1)}, f32[9,128]{1,0:T(8,128)S(1...) custom-call(s32[8,128]{1,0:T(8,128)} %cols_hbm.1, ...), custom_call_target="tpu_custom_call" | custom-call | tf_op jit(solution)/shard_map/first/pallas_call | solution.py:410
  2.4 16.1 %all_to_all.15 = f32[32,1,1536]{2,1,0:T(1,128)S(1)} all-to-all(f32[32,1,1536]{2,1,0:T(1,128)S(1)} %bitcast.12), channel_id=1, replica_groups=mesh['rows'=32] {'rows'}, dimensions={0} | all-to-all | bytes 393216 | tf_op jit(solution)/shard_map/all_to_all | solution.py:423
  18.5 1.2 %second.1 = (f32[160,128]{1,0:T(8,128)S(1)}, f32[9,128]{1,0:T(8,128)S(1)}, f32[9,128]{1,0:T(8,128)S(1)}, bf16[1024,128]{1,0:T(8,128)(2,1)S(1)}) custom-call(f32[384,128]{1,0:T(8,128)S(1)} %bitcast.10, f32[9,128]{1,0:T(8,128)S(1)} %get-tuple-element.22.rhs_ref, f32[9,128]{1,0:T(8,128)S(1)} %get-tuple-element.23.z_ref, ...), custom_call_target="tpu_custom_call" | custom-call | tf_op jit(solution)/shard_map/second/pallas_call | solution.py:410
  19.7 10.0 %all_to_all.16 = f32[32,1,640]{2,1,0:T(1,128)S(1)} all-to-all(f32[32,1,640]{2,1,0:T(1,128)S(1)} %bitcast.13), channel_id=1, replica_groups=mesh['rows'=32] {'rows'}, dimensions={0} | all-to-all | bytes 163840 | tf_op jit(solution)/shard_map/all_to_all | solution.py:423
  29.7 0.6 %third.1 = (f32[32,128]{1,0:T(8,128)S(1)}, f32[3,128]{1,0:T(4,128)S(1)}, f32[9,128]{1,0:T(8,128)S(1)}, f32[9,128]{1,0:T(8,128)S(1)}, f32[9,128]{1,0:T(8,128)S(1)}) custom-call(f32[160,128]{1,0:T(8,128)S(1)} %bitcast.11, f32[9,128]{1,0:T(8,128)S(1)} %get-tuple-element.22.rhs_ref, f32[9,128]{1,0:T(8,128)S(1)} %get-tuple-element.23.z_ref, ...), custom_call_target="tpu_custom_call" | custom-call | tf_op jit(solution)/shard_map/third/pallas_call | solution.py:410
  30.3 8.9 %all_to_all.17 = f32[32,1,128]{2,1,0:T(1,128)S(1)} all-to-all(f32[32,1,128]{2,1,0:T(1,128)S(1)} %bitcast.15), channel_id=1, replica_groups=mesh['rows'=32] {'rows'}, dimensions={0} | all-to-all | bytes 32768 | tf_op jit(solution)/shard_map/all_to_all | solution.py:423
  39.2 0.7 %fourth.1 = (f32[9,128]{1,0:T(8,128)}, f32[9,128]{1,0:T(8,128)}) custom-call(f32[32,128]{1,0:T(8,128)S(1)} %bitcast.14, f32[3,128]{1,0:T(4,128)S(1)} %get-tuple-element.36.known_ref, f32[9,128]{1,0:T(8,128)S(1)} %get-tuple-element.23.z_ref, f32[9,128]{1,0:T(8,128)S(1)} %get-tuple-element.32.q_ref, f32[9,128]{1,0:T(8,128)S(1)} %get-tuple-element.37.res_ref, ...), custom_call_target="tpu_custom_call" | custom-call | tf_op jit(solution)/shard_map/fourth/pallas_call | solution.py:410

commit v7 on v6

--- a/solution.py
+++ b/solution.py
@@ -123,6 +123,10 @@
     return jnp.sum(col_sum(x), axis=1, keepdims=True)
 
 
+def eight(x):
+    return sum(x[at : at + 8] for at in range(8, x.shape[0], 8)) + x[:8] if x.shape[0] > 8 else x
+
+
 def block_apply(sz, blocks_ref, v):
     acc = blocks_ref[0] * v[0:1]
     for b in range(1, sz.block):
@@ -145,7 +149,7 @@
     return jnp.concatenate(blocks, axis=1)
 
 
-def bucketed(sz, v, off, up_ref, chunk, lane_ref, val_ref):
+def bucketed(sz, v, off, up_ref, chunk, lane, val_ref):
     for b in range(sz.block):
         acc = up_ref[0, b] * v[0:1]
         for a in range(1, sz.block):
@@ -160,7 +164,7 @@
         jnp.where(where == jnp.full(parts.shape, at, BF16), parts, jnp.zeros(parts.shape, BF16))
         for at in range(sz.lists)
     ]
-    res = dot_t(jnp.concatenate(left, axis=0), side_by_side(lane_ref, sz.cams))
+    res = dot_t(jnp.concatenate(left, axis=0), lane)
     height = parts.shape[0]
     return [folded(res[at * height : (at + 1) * height]) for at in range(sz.lists)]
 
@@ -186,14 +190,16 @@
     for r in range(pk.rows):
         x = pk.read(msg_ref, r, sz.devices)
         for t in range(pk.groups):
-            turn_ref[r, t] = pltpu.roll(x, t * sz.refs, 1) if t else x
+            at = (r * pk.groups + t) * sz.devices
+            turn_ref[at : at + sz.devices, :] = pltpu.roll(x, t * sz.refs, 1) if t else x
     group = pk.group((sz.lists, sz.cams))
     out = []
     for v in range(pk.values):
         g, r = pk.at(v)
         value = None
         for s in range(pk.groups):
-            part = turn_ref[r, (s - g) % pk.groups, pl.ds(s, sz.lists, stride=pk.groups), :]
+            at = (r * pk.groups + (s - g) % pk.groups) * sz.devices + s
+            part = turn_ref[pl.ds(at, sz.lists, stride=pk.groups), :]
             value = part if value is None else jnp.where(group == s, part, value)
         out.append(value)
     return out
@@ -231,7 +237,7 @@
             at = 3 * high * b
             x = res[at : at + high] + res[at + high : at + 2 * high] + res[at + 2 * high :][:high]
             x = jnp.where(here, x, 0.0)
-            x = sum(x[i : i + 8] for i in range(0, high, 8))
+            x = eight(x)
             out[b] += [x[:, :c], x[:, c:]]
     return [row_sums(x) for x in out]
 
@@ -263,29 +269,25 @@
     copies = [pltpu.make_async_copy(a, b, sems.at[i]) for i, (a, b) in enumerate(pairs)]
     for copy in copies:
         copy.start()
-    for copy in copies[:4]:
+    for copy in copies[:2]:
         copy.wait()
     c = sz.cams
-    pk = sz.one
-    z = block_apply(sz, pre_ref, rhs_ref[...])
-    z_ref[...] = z
-    for b in range(sz.block):
-        at = pl.ds(b, sz.devices, stride=pk.stride)
-        msg_ref[at, :] = jnp.broadcast_to(z[b : b + 1], (sz.devices, c))
     cols = cols_ref[...]
     table = table_ref[...]
     height = table.shape[0]
     low = cols & (c - 1)
     high = cols >> sz.shift
     left = jnp.concatenate([table >> sz.shift, table & (c - 1)], axis=0).astype(F32).astype(BF16)
+    hot = jnp.concatenate([hot_rows(low[k : k + 1], (c, c)) for k in range(sz.lists)], axis=1)
+    res = dot(left, hot)
     owns, offs = [], []
     for k in range(sz.lists):
-        res = dot(left, hot_rows(low[k : k + 1], (c, c)))
         here = iota((height, c), 0) == high[k : k + 1]
-        owns.append(col_sum(jnp.where(here, res[:height], 0.0)))
-        offs.append(col_sum(jnp.where(here, res[height:], 0.0)))
-    own = jnp.concatenate(owns, axis=0).astype(I32)
-    off = jnp.concatenate(offs, axis=0).astype(I32)
+        lanes = slice(k * c, (k + 1) * c)
+        owns.append(eight(jnp.where(here, res[:height, lanes], 0.0)))
+        offs.append(eight(jnp.where(here, res[height:, lanes], 0.0)))
+    own = row_sums(owns).astype(I32)
+    off = row_sums(offs).astype(I32)
     own_ref[...] = own
     off_ref[...] = off
 
@@ -299,18 +301,26 @@
     places = []
     for k in range(sz.lists):
         part = counts[k * sz.devices : (k + 1) * sz.devices]
-        places.append(col_sum(hots[k] * (part[:, :c] + base)))
+        places.append(eight(hots[k] * (part[:, :c] + base)))
         base = base + part[:, c:]
-    pos = own * sz.refs + jnp.concatenate(places, axis=0).astype(I32)
+    pos = own * sz.refs + row_sums(places).astype(I32)
     chunk = pos >> sz.shift
     place = pos & (c - 1)
     chunk_ref[...] = chunk
+    lanes = [hot_rows(place[k : k + 1], (c, c)) for k in range(sz.lists)]
     for k in range(sz.lists):
-        lane_ref[k * c : (k + 1) * c, :] = hot_rows(place[k : k + 1], (c, c))
-
-    for copy in copies[4:]:
+        lane_ref[k * c : (k + 1) * c, :] = lanes[k]
+    lanes = jnp.concatenate(lanes, axis=1)
+
+    for copy in copies[2:]:
         copy.wait()
-    for at, x in enumerate(bucketed(sz, z, off, up_ref, chunk, lane_ref, val_ref)):
+    pk = sz.one
+    z = block_apply(sz, pre_ref, rhs_ref[...])
+    z_ref[...] = z
+    for b in range(sz.block):
+        at = pl.ds(b, sz.devices, stride=pk.stride)
+        msg_ref[at, :] = jnp.broadcast_to(z[b : b + 1], (sz.devices, c))
+    for at, x in enumerate(bucketed(sz, z, off, up_ref, chunk, lanes, val_ref)):
         tall_ref[at * TALL : (at + 1) * TALL, :] = x
     pack(sz, pk, lambda v: tall_ref[pl.ds(v, sz.lists, stride=TALL), :], msg_ref)
 
@@ -342,7 +352,8 @@
     answers = folded(dot(stacked(tall), side_by_side(hot_ref, c)))
     for at in range(sz.lists):
         ans_ref[at * TALL : (at + 1) * TALL, :] = answers[:, at * c : (at + 1) * c]
-    for at, x in enumerate(bucketed(sz, w, None, up_ref, chunk_ref[...], lane_ref, val_ref)):
+    lanes = side_by_side(lane_ref, c)
+    for at, x in enumerate(bucketed(sz, w, None, up_ref, chunk_ref[...], lanes, val_ref)):
         tall_ref[at * TALL : (at + 1) * TALL, :] = x
 
     def value_of(v):
@@ -436,7 +447,7 @@
     tall = pltpu.VMEM((lists * TALL, cams), F32)
 
     def turns(pk):
-        return pltpu.VMEM((pk.rows, pk.groups, sz.devices, cams), F32)
+        return pltpu.VMEM((pk.rows * pk.groups * sz.devices, cams), F32)
 
     ins = (block_cols, table, right_side, precond, upper_blocks, diag_blocks)
     msg, own, off, chunk, z, lane, right_side, precond, upper_blocks, diag_blocks = call(

time: 40.1 us -> 40 us (level)
  no operation moved by 1% of the time
where the time goes in v7:
time: 40 us; the launch traced here: 39.8 us
  blocking collectives  34.9 us (87%)
  Pallas kernels  4.18 us (10%)
  between operations  0.65 us (2%)
    all_to_all x3, blocking collectives, exchange(): lax.all_to_all(blocks, 'rows', split_axis=0, concat_axis=0, tiled=True)  34.9 us
    pallas_call x4, Pallas kernels, call(): pl.pallas_call(body, name=name, out_shape=[jax.ShapeDtypeStruct(s, t) for...  4.18 us

profile of v7, /device:TPU:0, one launch (start us, length us, event | category | flops | bytes accessed | tf_op | source)
XLA Modules:
  0.0 39.8 jit_solution(5263125314968356286)
XLA Ops:
  0.6 1.7 %first.1 = (f32[384,128]{1,0:T(8,128)S(1)}, s32[8,128]{1,0:T(8,128)S(1)}, s32[8,128]{1,0:T(8,128)S(1)}, s32[8,128]{1,0:T(8,128)S(1)}, f32[9,128]{1,0:T(8,128)S(1...) custom-call(s32[8,128]{1,0:T(8,128)} %cols_hbm.1, ...), custom_call_target="tpu_custom_call" | custom-call | tf_op jit(solution)/shard_map/first/pallas_call | solution.py:421
  2.3 16.1 %all_to_all.15 = f32[32,1,1536]{2,1,0:T(1,128)S(1)} all-to-all(f32[32,1,1536]{2,1,0:T(1,128)S(1)} %bitcast.12), channel_id=1, replica_groups=mesh['rows'=32] {'rows'}, dimensions={0} | all-to-all | bytes 393216 | tf_op jit(solution)/shard_map/all_to_all | solution.py:434
  18.4 1.2 %second.1 = (f32[160,128]{1,0:T(8,128)S(1)}, f32[9,128]{1,0:T(8,128)S(1)}, f32[9,128]{1,0:T(8,128)S(1)}, bf16[1024,128]{1,0:T(8,128)(2,1)S(1)}) custom-call(f32[384,128]{1,0:T(8,128)S(1)} %bitcast.10, f32[9,128]{1,0:T(8,128)S(1)} %get-tuple-element.22.rhs_ref, f32[9,128]{1,0:T(8,128)S(1)} %get-tuple-element.23.z_ref, ...), custom_call_target="tpu_custom_call" | custom-call | tf_op jit(solution)/shard_map/second/pallas_call | solution.py:421
  19.6 10.0 %all_to_all.16 = f32[32,1,640]{2,1,0:T(1,128)S(1)} all-to-all(f32[32,1,640]{2,1,0:T(1,128)S(1)} %bitcast.13), channel_id=1, replica_groups=mesh['rows'=32] {'rows'}, dimensions={0} | all-to-all | bytes 163840 | tf_op jit(solution)/shard_map/all_to_all | solution.py:434
  29.6 0.6 %third.1 = (f32[32,128]{1,0:T(8,128)S(1)}, f32[3,128]{1,0:T(4,128)S(1)}, f32[9,128]{1,0:T(8,128)S(1)}, f32[9,128]{1,0:T(8,128)S(1)}, f32[9,128]{1,0:T(8,128)S(1)}) custom-call(f32[160,128]{1,0:T(8,128)S(1)} %bitcast.11, f32[9,128]{1,0:T(8,128)S(1)} %get-tuple-element.22.rhs_ref, f32[9,128]{1,0:T(8,128)S(1)} %get-tuple-element.23.z_ref, ...), custom_call_target="tpu_custom_call" | custom-call | tf_op jit(solution)/shard_map/third/pallas_call | solution.py:421
  30.2 8.9 %all_to_all.17 = f32[32,1,128]{2,1,0:T(1,128)S(1)} all-to-all(f32[32,1,128]{2,1,0:T(1,128)S(1)} %bitcast.15), channel_id=1, replica_groups=mesh['rows'=32] {'rows'}, dimensions={0} | all-to-all | bytes 32768 | tf_op jit(solution)/shard_map/all_to_all | solution.py:434
  39.1 0.7 %fourth.1 = (f32[9,128]{1,0:T(8,128)}, f32[9,128]{1,0:T(8,128)}) custom-call(f32[32,128]{1,0:T(8,128)S(1)} %bitcast.14, f32[3,128]{1,0:T(4,128)S(1)} %get-tuple-element.36.known_ref, f32[9,128]{1,0:T(8,128)S(1)} %get-tuple-element.23.z_ref, f32[9,128]{1,0:T(8,128)S(1)} %get-tuple-element.32.q_ref, f32[9,128]{1,0:T(8,128)S(1)} %get-tuple-element.37.res_ref, ...), custom_call_target="tpu_custom_call" | custom-call | tf_op jit(solution)/shard_map/fourth/pallas_call | solution.py:421

commit v8 on v7

--- a/solution.py
+++ b/solution.py
@@ -47,7 +47,8 @@
         self.shift = cams.bit_length() - 1
         assert cams == 1 << self.shift and self.refs * devices == self.entries
         assert self.refs == 1 << (self.refs.bit_length() - 1) and lists <= 8
-        self.one = Packing(block + 1, self.refs, cams, block)
+        self.half = (block + 1) // 2
+        self.one = Packing(block + 1, self.refs, cams, self.half)
         self.two = Packing(2 * block + 1, self.refs, cams, 0)
         self.answer = block + 1
         assert self.answer % self.two.rows == 0
@@ -212,32 +213,37 @@
     return folded(dot_t(parts, side_by_side(hot_ref, sz.cams)))[: sz.block]
 
 
-def gather(sz, msg_ref, own, off):
-    c, stride = sz.cams, sz.one.stride
+def pick_owners(sz, own, off, pick_ref):
+    c = sz.cams
+    zeros = jnp.zeros((c, c), BF16)
+    for k in range(sz.lists):
+        hot = hot_rows(off[k : k + 1], (c, c))
+        low = jnp.broadcast_to((own[k : k + 1] & 3).astype(F32).astype(BF16), hot.shape)
+        for at in range(4):
+            row = (k * 4 + at) * c
+            pick_ref[row : row + c, :] = jnp.where(low == jnp.full(hot.shape, at, BF16), hot, zeros)
+
+
+def gather(sz, read, count, own, pick_ref):
+    c = sz.cams
     high = sz.devices // 4
     left = []
     for low in range(4):
         rows = []
-        for b in range(sz.block):
-            x = msg_ref[pl.ds(low * stride + b, high, stride=4 * stride), :]
-            rows += [p.astype(F32) for p in split3(x)]
+        for b in range(count):
+            rows += [p.astype(F32) for p in split3(read(b, low))]
         left.append(jnp.concatenate(rows, axis=0))
     left = jnp.concatenate(left, axis=1).astype(BF16)
-    out = [[] for _ in range(sz.block)]
-    zeros = jnp.zeros((c, 2 * c), BF16)
+    out = [[] for _ in range(count)]
     for k in range(0, sz.lists, 2):
-        pair = jnp.concatenate([off[k : k + 1], off[k + 1 : k + 2]], axis=1)
         owner = jnp.concatenate([own[k : k + 1], own[k + 1 : k + 2]], axis=1)
-        hot = hot_rows(pair, (c, 2 * c))
-        low = jnp.broadcast_to((owner & 3).astype(F32).astype(BF16), hot.shape)
-        right = [jnp.where(low == jnp.full(hot.shape, at, BF16), hot, zeros) for at in range(4)]
-        res = dot(left, jnp.concatenate(right, axis=0))
+        right = [pick_ref[at * 4 * c : (at + 1) * 4 * c, :] for at in (k, k + 1)]
+        res = dot(left, jnp.concatenate(right, axis=1))
         here = iota((high, 2 * c), 0) == (owner >> 2)
-        for b in range(sz.block):
+        for b in range(count):
             at = 3 * high * b
             x = res[at : at + high] + res[at + high : at + 2 * high] + res[at + 2 * high :][:high]
-            x = jnp.where(here, x, 0.0)
-            x = eight(x)
+            x = eight(jnp.where(here, x, 0.0))
             out[b] += [x[:, :c], x[:, c:]]
     return [row_sums(x) for x in out]
 
@@ -317,27 +323,60 @@
     pk = sz.one
     z = block_apply(sz, pre_ref, rhs_ref[...])
     z_ref[...] = z
-    for b in range(sz.block):
-        at = pl.ds(b, sz.devices, stride=pk.stride)
-        msg_ref[at, :] = jnp.broadcast_to(z[b : b + 1], (sz.devices, c))
+    for r in range(sz.half):
+        for core in range(2):
+            row = r + core * (sz.block - sz.half)
+            at = pl.ds(core * pk.stride + r, sz.devices // 2, stride=2 * pk.stride)
+            msg_ref[at, :] = jnp.broadcast_to(z[row : row + 1], (sz.devices // 2, c))
     for at, x in enumerate(bucketed(sz, z, off, up_ref, chunk, lanes, val_ref)):
         tall_ref[at * TALL : (at + 1) * TALL, :] = x
     pack(sz, pk, lambda v: tall_ref[pl.ds(v, sz.lists, stride=TALL), :], msg_ref)
 
 
-def second_kernel(
-    sz, got_ref, rhs_ref, z_ref, own_ref, off_ref, chunk_ref, lane_ref, diag_ref, pre_ref, up_ref,
-    msg_ref, q_ref, side_ref, hot_ref,
-    val_ref, tall_ref, ans_ref, turn_ref,
+def meanwhile_kernel(
+    sz, got_ref, own_ref, off_ref,
+    pushed_ref, hot_ref, mine_ref, pick_ref,
+    val_ref, turn_ref,
 ):
-    c = sz.cams
-    b, z = rhs_ref[...], z_ref[...]
+    c, stride = sz.cams, sz.one.stride
+    own = own_ref[...]
     values = unpack(sz, sz.one, got_ref, turn_ref)
     wanted = values[sz.block].astype(I32)
     for at in range(sz.lists):
         hot_ref[at * c : (at + 1) * c, :] = hot_rows(wanted[at : at + 1], (c, c))
-    pushed = scatter(sz, values, val_ref, hot_ref)
-    gathered = gather(sz, got_ref, own_ref[...], off_ref[...])
+    pushed_ref[...] = scatter(sz, values, val_ref, hot_ref)
+    pick_owners(sz, own, off_ref[...], pick_ref)
+
+    def read(b, low):
+        return got_ref[pl.ds(low * stride + b, sz.devices // 4, stride=4 * stride), :]
+
+    for b, x in enumerate(gather(sz, read, sz.half, own, pick_ref)):
+        mine_ref[b * sz.lists : (b + 1) * sz.lists, :] = x
+
+
+def second_kernel(
+    sz, near_ref, pushed_ref, hot_ref, mine_ref, pick_ref, rhs_ref, z_ref, own_ref, chunk_ref,
+    lane_ref, diag_ref, pre_ref, up_ref,
+    msg_ref, q_ref, side_ref,
+    val_ref, tall_ref, ans_ref,
+):
+    c, stride = sz.cams, sz.one.stride
+    b, z = rhs_ref[...], z_ref[...]
+    pushed = pushed_ref[...]
+    odd = (lax.axis_index("rows") & 1) == 1
+    rest = sz.block - sz.half
+    shift = sz.half - rest
+
+    def read(row, low):
+        first, later = [
+            near_ref[pl.ds(low * stride + at, sz.devices // 4, stride=4 * stride), :]
+            for at in (row, row + shift)
+        ]
+        return jnp.where(odd, first, later)
+
+    near = gather(sz, read, rest, own_ref[...], pick_ref)
+    mine = [mine_ref[at * sz.lists : (at + 1) * sz.lists, :] for at in range(sz.half)]
+    gathered = [jnp.where(odd, x, y) for x, y in zip(near + mine, mine + near)]
     side = upper_apply(sz, up_ref, gathered) + pushed
     q = block_apply(sz, diag_ref, z) + side
     w = block_apply(sz, pre_ref, q)
@@ -417,7 +456,7 @@
     left_ref[...] = res_ref[...] - next_step * (img_ref[...] + beta * q_ref[...])
 
 
-def call(body, name, outs, scratch, *args, space=pltpu.VMEM):
+def call(body, name, outs, scratch, *args, space=pltpu.VMEM, cost=0):
     return pl.pallas_call(
         body,
         name=name,
@@ -426,6 +465,7 @@
         out_specs=[pl.BlockSpec(memory_space=pltpu.VMEM)] * len(outs),
         scratch_shapes=scratch,
         compiler_params=pltpu.CompilerParams(vmem_limit_bytes=VMEM),
+        cost_estimate=pl.CostEstimate(flops=cost, bytes_accessed=cost, transcendentals=0),
     )(*args)
 
 
@@ -459,11 +499,20 @@
         *(pltpu.with_memory_space_constraint(x, pltpu.HBM) for x in ins), space=pltpu.HBM,
     )
     got = exchange(sz, msg, sz.one.stride)
-    msg, q, side, hot = call(
+    cores = [(i, i ^ 1) for i in range(sz.devices)]
+    near = lax.ppermute(got, "rows", cores)
+    pushed, hot, mine, pick = call(
+        functools.partial(meanwhile_kernel, sz), "meanwhile",
+        [field, hot_type, ((sz.half * lists, cams), F32), ((4 * sz.entries, cams), BF16)],
+        [tall, turns(sz.one)],
+        got, own, off, cost=4_000_000,
+    )
+    msg, q, side = call(
         functools.partial(second_kernel, sz), "second",
-        [((sz.devices * sz.two.stride, cams), F32), field, field, hot_type],
-        [tall] * 3 + [turns(sz.one)],
-        got, right_side, z, own, off, chunk, lane, diag_blocks, precond, upper_blocks,
+        [((sz.devices * sz.two.stride, cams), F32), field, field],
+        [tall] * 3,
+        near, pushed, hot, mine, pick, right_side, z, own, chunk, lane, diag_blocks, precond,
+        upper_blocks,
     )
     got = exchange(sz, msg, sz.two.stride)
     part, known, res, pre, image = call(

time: 40 us -> 39.7 us (level)
  blocking collectives: 34.9 us -> 33.5 us
  waiting for transfers between devices: 0 us -> 0.57 us
    all_to_all x3, blocking collectives: 34.9 us -> 33.5 us  [exchange(): lax.all_to_all(blocks, 'rows', split_axis=0, concat_axis=0, tiled=True)]
    ppermute x0 -> x1, waiting for transfers between devices: none -> 0.57 us  [local(): near = lax.ppermute(got, 'rows', cores)]
    pallas_call x4 -> x5, Pallas kernels: 4.18 us -> 4.43 us  [call(): pl.pallas_call(body, name=name, out_shape=[jax.ShapeDtypeStruct(s, t) for...]
  transfers between devices with their start and end apart: 0 -> 1, of which waited for: 0 -> 1; matrix products, arithmetic and copies ran while one was open for 0% -> 0% of each run, Pallas kernels for 0% -> 1%
where the time goes in v8:
time: 39.7 us; the launch traced here: 39.4 us
  blocking collectives  33.5 us (84%)
  Pallas kernels  4.43 us (11%)
  between operations  0.66 us (2%)
  waiting for transfers between devices  0.57 us (1%)
    all_to_all x3, blocking collectives, exchange(): lax.all_to_all(blocks, 'rows', split_axis=0, concat_axis=0, tiled=True)  33.5 us
    pallas_call x5, Pallas kernels, call(): pl.pallas_call(body, name=name, out_shape=[jax.ShapeDtypeStruct(s, t) for...  4.43 us
  transfers between devices with their start and end apart: 1, of which 1 were waited for; matrix products, arithmetic and copies ran while one was open for 0% of the time, Pallas kernels for 1%

profile of v8, /device:TPU:0, one launch (start us, length us, event | category | flops | bytes accessed | tf_op | source)
XLA Modules:
  0.0 39.4 jit_solution(6419454334665642490)
XLA Ops:
  0.6 1.7 %first.1 = (f32[256,128]{1,0:T(8,128)S(1)}, s32[8,128]{1,0:T(8,128)S(1)}, s32[8,128]{1,0:T(8,128)S(1)}, s32[8,128]{1,0:T(8,128)S(1)}, f32[9,128]{1,0:T(8,128)S(1...) custom-call(s32[8,128]{1,0:T(8,128)} %cols_hbm.1, ...), custom_call_target="tpu_custom_call" | custom-call | tf_op jit(solution)/shard_map/first/pallas_call | solution.py:460
  2.4 15.3 %all_to_all.15 = f32[32,1,1024]{2,1,0:T(1,128)S(1)} all-to-all(f32[32,1,1024]{2,1,0:T(1,128)S(1)} %bitcast.13), channel_id=1, replica_groups=mesh['rows'=32] {'rows'}, dimensions={0} | all-to-all | bytes 262144 | tf_op jit(solution)/shard_map/all_to_all | solution.py:474
  17.7 0.2 collective-permute-start
  17.9 0.6 %meanwhile.1 = (f32[9,128]{1,0:T(8,128)S(1)}, bf16[1024,128]{1,0:T(8,128)(2,1)S(1)}, f32[40,128]{1,0:T(8,128)S(1)}, bf16[4096,128]{1,0:T(8,128)(2,1)S(1)}) custom-call(f32[256,128]{1,0:T(8,128)S(1)} %bitcast.11, s32[8,128]{1,0:T(8,128)S(1)} %get-tuple-element.25.own_ref, s32[8,128]{1,0:T(8,128)S(1)} %get-tuple-element.26.off_ref), custom_call_target="tpu_custom_call" | custom-call | flops 4000000 | bytes 4000000 | tf_op jit(solution)/shard_map/meanwhile/pallas_call | solution.py:460
  18.5 0.6 %collective-permute-done.near_ref = f32[256,128]{1,0:T(8,128)S(1)} collective-permute-done((f32[256,128]{1,0:T(8,128)S(1)}, f32[256,128]{1,0:T(8,128)S(1)}, u32[]{:S(2)}, u32[]{:S(2)}) %collective-permute-start) | collective-permute-done | bytes 131104 | tf_op jit(solution)/shard_map/ppermute | solution.py:503
  19.0 0.9 %second.1 = (f32[160,128]{1,0:T(8,128)S(1)}, f32[9,128]{1,0:T(8,128)S(1)}, f32[9,128]{1,0:T(8,128)S(1)}) custom-call(f32[256,128]{1,0:T(8,128)S(1)} %collective-permute-done.near_ref, f32[9,128]{1,0:T(8,128)S(1)} %get-tuple-element.27.pushed_ref, bf16[1024,128]{1,0:T(8,128)(2,1)S(1)} %get-tuple-element.28.hot_ref, f32[40,128]{1,0:T(8,128)S(1)} %get-tuple-element.29.mine_ref, ...), custom_call_target="tpu_custom_call" | custom-call | tf_op jit(solution)/shard_map/second/pallas_call | solution.py:460
  19.9 9.3 %all_to_all.16 = f32[32,1,640]{2,1,0:T(1,128)S(1)} all-to-all(f32[32,1,640]{2,1,0:T(1,128)S(1)} %bitcast.14), channel_id=1, replica_groups=mesh['rows'=32] {'rows'}, dimensions={0} | all-to-all | bytes 163840 | tf_op jit(solution)/shard_map/all_to_all | solution.py:474
  29.3 0.6 %third.1 = (f32[32,128]{1,0:T(8,128)S(1)}, f32[3,128]{1,0:T(4,128)S(1)}, f32[9,128]{1,0:T(8,128)S(1)}, f32[9,128]{1,0:T(8,128)S(1)}, f32[9,128]{1,0:T(8,128)S(1)}) custom-call(f32[160,128]{1,0:T(8,128)S(1)} %bitcast.12, f32[9,128]{1,0:T(8,128)S(1)} %get-tuple-element.31.rhs_ref, f32[9,128]{1,0:T(8,128)S(1)} %get-tuple-element.32.z_ref, ...), custom_call_target="tpu_custom_call" | custom-call | tf_op jit(solution)/shard_map/third/pallas_call | solution.py:460
  29.9 8.9 %all_to_all.17 = f32[32,1,128]{2,1,0:T(1,128)S(1)} all-to-all(f32[32,1,128]{2,1,0:T(1,128)S(1)} %bitcast.16), channel_id=1, replica_groups=mesh['rows'=32] {'rows'}, dimensions={0} | all-to-all | bytes 32768 | tf_op jit(solution)/shard_map/all_to_all | solution.py:474
  38.7 0.7 %fourth.1 = (f32[9,128]{1,0:T(8,128)}, f32[9,128]{1,0:T(8,128)}) custom-call(f32[32,128]{1,0:T(8,128)S(1)} %bitcast.15, f32[3,128]{1,0:T(4,128)S(1)} %get-tuple-element.42.known_ref, f32[9,128]{1,0:T(8,128)S(1)} %get-tuple-element.32.z_ref, f32[9,128]{1,0:T(8,128)S(1)} %get-tuple-element.39.q_ref, f32[9,128]{1,0:T(8,128)S(1)} %get-tuple-element.43.res_ref, ...), custom_call_target="tpu_custom_call" | custom-call | tf_op jit(solution)/shard_map/fourth/pallas_call | solution.py:460
Async XLA Ops:
  17.7 1.3 %collective-permute-start = (f32[256,128]{1,0:T(8,128)S(1)}, f32[256,128]{1,0:T(8,128)S(1)}, u32[]{:S(2)}, u32[]{:S(2)}) collective-permute-start(f32[256,128]{1,0:T(8,128)S(1)} %bitcast.10), channel_id=1, source_target_pairs={{0,1},{1,0},{2,3},{3,2},{4,5},{5,4},{6,7},{7,6},{8,9},{9,8},{10,11... | collective-permute-start | bytes 393224 | tf_op jit(solution)/shard_map/ppermute | solution.py:503

commit v9 on v8

--- a/solution.py
+++ b/solution.py
@@ -135,13 +135,18 @@
     return acc
 
 
-def upper_apply(sz, up_ref, gathered):
+def upper_apply(sz, up_ref, gathered, start=0, partial=None):
     rows = []
     for a in range(sz.block):
-        acc = up_ref[a, 0] * gathered[0]
-        for b in range(1, sz.block):
-            acc = acc + up_ref[a, b] * gathered[b]
+        acc = None if partial is None else partial[a]
+        for i, x in enumerate(gathered):
+            term = up_ref[a, start + i] * x
+            acc = term if acc is None else acc + term
         rows.append(acc)
+    return rows
+
+
+def list_sums(rows):
     return jnp.concatenate([row_sums(rows[:8])] + [col_sum(x) for x in rows[8:]], axis=0)
 
 
@@ -334,8 +339,8 @@
 
 
 def meanwhile_kernel(
-    sz, got_ref, own_ref, off_ref,
-    pushed_ref, hot_ref, mine_ref, pick_ref,
+    sz, got_ref, own_ref, off_ref, rhs_ref, z_ref, diag_ref, up_ref,
+    pushed_ref, hot_ref, mine_ref, pick_ref, part_ref, dot_ref,
     val_ref, turn_ref,
 ):
     c, stride = sz.cams, sz.one.stride
@@ -350,19 +355,23 @@
     def read(b, low):
         return got_ref[pl.ds(low * stride + b, sz.devices // 4, stride=4 * stride), :]
 
-    for b, x in enumerate(gather(sz, read, sz.half, own, pick_ref)):
-        mine_ref[b * sz.lists : (b + 1) * sz.lists, :] = x
+    start = (lax.axis_index("rows") & 1) * (sz.block - sz.half)
+    mine = gather(sz, read, sz.half, own, pick_ref)
+    for a, x in enumerate(upper_apply(sz, up_ref, mine, start)):
+        mine_ref[a * sz.lists : (a + 1) * sz.lists, :] = x
+    z = z_ref[...]
+    part_ref[...] = block_apply(sz, diag_ref, z)
+    dot_ref[...] = jnp.broadcast_to(total(rhs_ref[...] * z), dot_ref.shape)
 
 
 def second_kernel(
-    sz, near_ref, pushed_ref, hot_ref, mine_ref, pick_ref, rhs_ref, z_ref, own_ref, chunk_ref,
-    lane_ref, diag_ref, pre_ref, up_ref,
+    sz, near_ref, pushed_ref, hot_ref, mine_ref, pick_ref, dot_ref, z_ref, own_ref, chunk_ref,
+    lane_ref, part_ref, pre_ref, up_ref,
     msg_ref, q_ref, side_ref,
     val_ref, tall_ref, ans_ref,
 ):
     c, stride = sz.cams, sz.one.stride
-    b, z = rhs_ref[...], z_ref[...]
-    pushed = pushed_ref[...]
+    z = z_ref[...]
     odd = (lax.axis_index("rows") & 1) == 1
     rest = sz.block - sz.half
     shift = sz.half - rest
@@ -375,14 +384,15 @@
         return jnp.where(odd, first, later)
 
     near = gather(sz, read, rest, own_ref[...], pick_ref)
-    mine = [mine_ref[at * sz.lists : (at + 1) * sz.lists, :] for at in range(sz.half)]
-    gathered = [jnp.where(odd, x, y) for x, y in zip(near + mine, mine + near)]
-    side = upper_apply(sz, up_ref, gathered) + pushed
-    q = block_apply(sz, diag_ref, z) + side
+    mine = [mine_ref[at * sz.lists : (at + 1) * sz.lists, :] for at in range(sz.block)]
+    start = (1 - (lax.axis_index("rows") & 1)) * sz.half
+    upper = list_sums(upper_apply(sz, up_ref, near, start, mine))
+    side = upper + pushed_ref[...]
+    q = part_ref[...] + side
     w = block_apply(sz, pre_ref, q)
     q_ref[...] = q
     side_ref[...] = side
-    dots = [total(b * z), total(z * q)]
+    dots = [dot_ref[...], total(z * q)]
     lane = iota((sz.lists, c), 1) & (sz.refs - 1)
     dot_rows = jnp.zeros((sz.lists, c), F32)
     for at, d in enumerate(dots):
@@ -425,7 +435,7 @@
         sz, values[sz.answer :], chunk_ref[...], lane_ref, tall_ref, col_ref
     )
     pushed = scatter(sz, values, val_ref, hot_ref)
-    side = side_ref[...] - step * (upper_apply(sz, up_ref, gathered) + pushed)
+    side = side_ref[...] - step * (list_sums(upper_apply(sz, up_ref, gathered)) + pushed)
     image = block_apply(sz, diag_ref, pre) + side
     res_ref[...] = residual
     dir_ref[...] = pre
@@ -501,17 +511,18 @@
     got = exchange(sz, msg, sz.one.stride)
     cores = [(i, i ^ 1) for i in range(sz.devices)]
     near = lax.ppermute(got, "rows", cores)
-    pushed, hot, mine, pick = call(
+    pushed, hot, mine, pick, part, bz = call(
         functools.partial(meanwhile_kernel, sz), "meanwhile",
-        [field, hot_type, ((sz.half * lists, cams), F32), ((4 * sz.entries, cams), BF16)],
+        [field, hot_type, ((block * lists, cams), F32), ((4 * sz.entries, cams), BF16),
+         field, ((1, cams), F32)],
         [tall, turns(sz.one)],
-        got, own, off, cost=4_000_000,
+        got, own, off, right_side, z, diag_blocks, upper_blocks, cost=4_000_000,
     )
     msg, q, side = call(
         functools.partial(second_kernel, sz), "second",
         [((sz.devices * sz.two.stride, cams), F32), field, field],
         [tall] * 3,
-        near, pushed, hot, mine, pick, right_side, z, own, chunk, lane, diag_blocks, precond,
+        near, pushed, hot, mine, pick, bz, z, own, chunk, lane, part, precond,
         upper_blocks,
     )
     got = exchange(sz, msg, sz.two.stride)

time: 39.7 us -> 39.7 us (level)
  no operation moved by 1% of the time
where the time goes in v9:
time: 39.7 us; the launch traced here: 39.4 us
  blocking collectives  33.5 us (84%)
  Pallas kernels  4.43 us (11%)
  between operations  0.66 us (2%)
  waiting for transfers between devices  0.55 us (1%)
    all_to_all x3, blocking collectives, exchange(): lax.all_to_all(blocks, 'rows', split_axis=0, concat_axis=0, tiled=True)  33.5 us
    pallas_call x5, Pallas kernels, call(): pl.pallas_call(body, name=name, out_shape=[jax.ShapeDtypeStruct(s, t) for...  4.43 us
  transfers between devices with their start and end apart: 1, of which 1 were waited for; matrix products, arithmetic and copies ran while one was open for 0% of the time, Pallas kernels for 1%

profile of v9, /device:TPU:0, one launch (start us, length us, event | category | flops | bytes accessed | tf_op | source)
XLA Modules:
  0.0 39.4 jit_solution(3419134042485187798)
XLA Ops:
  0.6 1.7 %first.1 = (f32[256,128]{1,0:T(8,128)S(1)}, s32[8,128]{1,0:T(8,128)S(1)}, s32[8,128]{1,0:T(8,128)S(1)}, s32[8,128]{1,0:T(8,128)S(1)}, f32[9,128]{1,0:T(8,128)S(1...) custom-call(s32[8,128]{1,0:T(8,128)} %cols_hbm.1, ...), custom_call_target="tpu_custom_call" | custom-call | tf_op jit(solution)/shard_map/first/pallas_call | solution.py:470
  2.4 15.3 %all_to_all.15 = f32[32,1,1024]{2,1,0:T(1,128)S(1)} all-to-all(f32[32,1,1024]{2,1,0:T(1,128)S(1)} %bitcast.13), channel_id=1, replica_groups=mesh['rows'=32] {'rows'}, dimensions={0} | all-to-all | bytes 262144 | tf_op jit(solution)/shard_map/all_to_all | solution.py:484
  17.7 0.2 collective-permute-start
  17.9 0.6 %meanwhile.1 = (f32[9,128]{1,0:T(8,128)S(1)}, bf16[1024,128]{1,0:T(8,128)(2,1)S(1)}, f32[72,128]{1,0:T(8,128)S(1)}, bf16[4096,128]{1,0:T(8,128)(2,1)S(1)}, f32[9,128]{1,0:T(8,128)S(1)}, /*index=5*/f32[1,128]{1,0:T(1,128)S(1)}) custom-call(f32[256,128]{1,0:T(8,128)S(1)} %bitcast.11, s32[8,128]{1,0:T(8,128)S(1)} %get-tuple-element.27.own_ref, ...), custom_call_target="tpu_custom_call" | custom-call | flops 4000000 | bytes 4000000 | tf_op jit(solution)/shard_map/meanwhile/pallas_call | solution.py:470
  18.5 0.6 %collective-permute-done.near_ref = f32[256,128]{1,0:T(8,128)S(1)} collective-permute-done((f32[256,128]{1,0:T(8,128)S(1)}, f32[256,128]{1,0:T(8,128)S(1)}, u32[]{:S(2)}, u32[]{:S(2)}) %collective-permute-start) | collective-permute-done | bytes 131104 | tf_op jit(solution)/shard_map/ppermute | solution.py:513
  19.0 0.8 %second.1 = (f32[160,128]{1,0:T(8,128)S(1)}, f32[9,128]{1,0:T(8,128)S(1)}, f32[9,128]{1,0:T(8,128)S(1)}) custom-call(f32[256,128]{1,0:T(8,128)S(1)} %collective-permute-done.near_ref, f32[9,128]{1,0:T(8,128)S(1)} %get-tuple-element.33.pushed_ref, bf16[1024,128]{1,0:T(8,128)(2,1)S(1)} %get-tuple-element.34.hot_ref, f32[72,128]{1,0:T(8,128)S(1)} %get-tuple-element.35.mine_ref, ...), custom_call_target="tpu_custom_call" | custom-call | tf_op jit(solution)/shard_map/second/pallas_call | solution.py:470
  19.9 9.3 %all_to_all.16 = f32[32,1,640]{2,1,0:T(1,128)S(1)} all-to-all(f32[32,1,640]{2,1,0:T(1,128)S(1)} %bitcast.14), channel_id=1, replica_groups=mesh['rows'=32] {'rows'}, dimensions={0} | all-to-all | bytes 163840 | tf_op jit(solution)/shard_map/all_to_all | solution.py:484
  29.2 0.6 %third.1 = (f32[32,128]{1,0:T(8,128)S(1)}, f32[3,128]{1,0:T(4,128)S(1)}, f32[9,128]{1,0:T(8,128)S(1)}, f32[9,128]{1,0:T(8,128)S(1)}, f32[9,128]{1,0:T(8,128)S(1)}) custom-call(f32[160,128]{1,0:T(8,128)S(1)} %bitcast.12, f32[9,128]{1,0:T(8,128)S(1)} %get-tuple-element.29.rhs_ref, f32[9,128]{1,0:T(8,128)S(1)} %get-tuple-element.30.z_ref, ...), custom_call_target="tpu_custom_call" | custom-call | tf_op jit(solution)/shard_map/third/pallas_call | solution.py:470
  29.8 8.9 %all_to_all.17 = f32[32,1,128]{2,1,0:T(1,128)S(1)} all-to-all(f32[32,1,128]{2,1,0:T(1,128)S(1)} %bitcast.16), channel_id=1, replica_groups=mesh['rows'=32] {'rows'}, dimensions={0} | all-to-all | bytes 32768 | tf_op jit(solution)/shard_map/all_to_all | solution.py:484
  38.7 0.7 %fourth.1 = (f32[9,128]{1,0:T(8,128)}, f32[9,128]{1,0:T(8,128)}) custom-call(f32[32,128]{1,0:T(8,128)S(1)} %bitcast.15, f32[3,128]{1,0:T(4,128)S(1)} %get-tuple-element.46.known_ref, f32[9,128]{1,0:T(8,128)S(1)} %get-tuple-element.30.z_ref, f32[9,128]{1,0:T(8,128)S(1)} %get-tuple-element.43.q_ref, f32[9,128]{1,0:T(8,128)S(1)} %get-tuple-element.47.res_ref, ...), custom_call_target="tpu_custom_call" | custom-call | tf_op jit(solution)/shard_map/fourth/pallas_call | solution.py:470
Async XLA Ops:
  17.7 1.3 %collective-permute-start = (f32[256,128]{1,0:T(8,128)S(1)}, f32[256,128]{1,0:T(8,128)S(1)}, u32[]{:S(2)}, u32[]{:S(2)}) collective-permute-start(f32[256,128]{1,0:T(8,128)S(1)} %bitcast.10), channel_id=1, source_target_pairs={{0,1},{1,0},{2,3},{3,2},{4,5},{5,4},{6,7},{7,6},{8,9},{9,8},{10,11... | collective-permute-start | bytes 393224 | tf_op jit(solution)/shard_map/ppermute | solution.py:513

commit v10 on v9

--- a/solution.py
+++ b/solution.py
@@ -372,20 +372,16 @@
 ):
     c, stride = sz.cams, sz.one.stride
     z = z_ref[...]
-    odd = (lax.axis_index("rows") & 1) == 1
+    even = 1 - (lax.axis_index("rows") & 1)
     rest = sz.block - sz.half
-    shift = sz.half - rest
+    skip = even * (sz.half - rest)
 
     def read(row, low):
-        first, later = [
-            near_ref[pl.ds(low * stride + at, sz.devices // 4, stride=4 * stride), :]
-            for at in (row, row + shift)
-        ]
-        return jnp.where(odd, first, later)
+        return near_ref[pl.ds(low * stride + row + skip, sz.devices // 4, stride=4 * stride), :]
 
     near = gather(sz, read, rest, own_ref[...], pick_ref)
     mine = [mine_ref[at * sz.lists : (at + 1) * sz.lists, :] for at in range(sz.block)]
-    start = (1 - (lax.axis_index("rows") & 1)) * sz.half
+    start = even * sz.half
     upper = list_sums(upper_apply(sz, up_ref, near, start, mine))
     side = upper + pushed_ref[...]
     q = part_ref[...] + side

time: 39.7 us -> 39.6 us (level)
  no operation moved by 1% of the time
where the time goes in v10:
time: 39.6 us; the launch traced here: 39.4 us
  blocking collectives  33.5 us (85%)
  Pallas kernels  4.42 us (11%)
  between operations  0.66 us (2%)
  waiting for transfers between devices  0.55 us (1%)
    all_to_all x3, blocking collectives, exchange(): lax.all_to_all(blocks, 'rows', split_axis=0, concat_axis=0, tiled=True)  33.5 us
    pallas_call x5, Pallas kernels, call(): pl.pallas_call(body, name=name, out_shape=[jax.ShapeDtypeStruct(s, t) for...  4.42 us
  transfers between devices with their start and end apart: 1, of which 1 were waited for; matrix products, arithmetic and copies ran while one was open for 0% of the time, Pallas kernels for 1%

profile of v10, /device:TPU:0, one launch (start us, length us, event | category | flops | bytes accessed | tf_op | source)
XLA Modules:
  0.0 39.4 jit_solution(7726192012979065834)
XLA Ops:
  0.6 1.7 %first.1 = (f32[256,128]{1,0:T(8,128)S(1)}, s32[8,128]{1,0:T(8,128)S(1)}, s32[8,128]{1,0:T(8,128)S(1)}, s32[8,128]{1,0:T(8,128)S(1)}, f32[9,128]{1,0:T(8,128)S(1...) custom-call(s32[8,128]{1,0:T(8,128)} %cols_hbm.1, ...), custom_call_target="tpu_custom_call" | custom-call | tf_op jit(solution)/shard_map/first/pallas_call | solution.py:466
  2.4 15.3 %all_to_all.15 = f32[32,1,1024]{2,1,0:T(1,128)S(1)} all-to-all(f32[32,1,1024]{2,1,0:T(1,128)S(1)} %bitcast.13), channel_id=1, replica_groups=mesh['rows'=32] {'rows'}, dimensions={0} | all-to-all | bytes 262144 | tf_op jit(solution)/shard_map/all_to_all | solution.py:480
  17.7 0.2 collective-permute-start
  17.9 0.6 %meanwhile.1 = (f32[9,128]{1,0:T(8,128)S(1)}, bf16[1024,128]{1,0:T(8,128)(2,1)S(1)}, f32[72,128]{1,0:T(8,128)S(1)}, bf16[4096,128]{1,0:T(8,128)(2,1)S(1)}, f32[9,128]{1,0:T(8,128)S(1)}, /*index=5*/f32[1,128]{1,0:T(1,128)S(1)}) custom-call(f32[256,128]{1,0:T(8,128)S(1)} %bitcast.11, s32[8,128]{1,0:T(8,128)S(1)} %get-tuple-element.27.own_ref, ...), custom_call_target="tpu_custom_call" | custom-call | flops 4000000 | bytes 4000000 | tf_op jit(solution)/shard_map/meanwhile/pallas_call | solution.py:466
  18.5 0.6 %collective-permute-done.near_ref = f32[256,128]{1,0:T(8,128)S(1)} collective-permute-done((f32[256,128]{1,0:T(8,128)S(1)}, f32[256,128]{1,0:T(8,128)S(1)}, u32[]{:S(2)}, u32[]{:S(2)}) %collective-permute-start) | collective-permute-done | bytes 131104 | tf_op jit(solution)/shard_map/ppermute | solution.py:509
  19.0 0.8 %second.1 = (f32[160,128]{1,0:T(8,128)S(1)}, f32[9,128]{1,0:T(8,128)S(1)}, f32[9,128]{1,0:T(8,128)S(1)}) custom-call(f32[256,128]{1,0:T(8,128)S(1)} %collective-permute-done.near_ref, f32[9,128]{1,0:T(8,128)S(1)} %get-tuple-element.33.pushed_ref, bf16[1024,128]{1,0:T(8,128)(2,1)S(1)} %get-tuple-element.34.hot_ref, f32[72,128]{1,0:T(8,128)S(1)} %get-tuple-element.35.mine_ref, ...), custom_call_target="tpu_custom_call" | custom-call | tf_op jit(solution)/shard_map/second/pallas_call | solution.py:466
  19.9 9.3 %all_to_all.16 = f32[32,1,640]{2,1,0:T(1,128)S(1)} all-to-all(f32[32,1,640]{2,1,0:T(1,128)S(1)} %bitcast.14), channel_id=1, replica_groups=mesh['rows'=32] {'rows'}, dimensions={0} | all-to-all | bytes 163840 | tf_op jit(solution)/shard_map/all_to_all | solution.py:480
  29.2 0.6 %third.1 = (f32[32,128]{1,0:T(8,128)S(1)}, f32[3,128]{1,0:T(4,128)S(1)}, f32[9,128]{1,0:T(8,128)S(1)}, f32[9,128]{1,0:T(8,128)S(1)}, f32[9,128]{1,0:T(8,128)S(1)}) custom-call(f32[160,128]{1,0:T(8,128)S(1)} %bitcast.12, f32[9,128]{1,0:T(8,128)S(1)} %get-tuple-element.29.rhs_ref, f32[9,128]{1,0:T(8,128)S(1)} %get-tuple-element.30.z_ref, ...), custom_call_target="tpu_custom_call" | custom-call | tf_op jit(solution)/shard_map/third/pallas_call | solution.py:466
  29.8 8.9 %all_to_all.17 = f32[32,1,128]{2,1,0:T(1,128)S(1)} all-to-all(f32[32,1,128]{2,1,0:T(1,128)S(1)} %bitcast.16), channel_id=1, replica_groups=mesh['rows'=32] {'rows'}, dimensions={0} | all-to-all | bytes 32768 | tf_op jit(solution)/shard_map/all_to_all | solution.py:480
  38.7 0.7 %fourth.1 = (f32[9,128]{1,0:T(8,128)}, f32[9,128]{1,0:T(8,128)}) custom-call(f32[32,128]{1,0:T(8,128)S(1)} %bitcast.15, f32[3,128]{1,0:T(4,128)S(1)} %get-tuple-element.46.known_ref, f32[9,128]{1,0:T(8,128)S(1)} %get-tuple-element.30.z_ref, f32[9,128]{1,0:T(8,128)S(1)} %get-tuple-element.43.q_ref, f32[9,128]{1,0:T(8,128)S(1)} %get-tuple-element.47.res_ref, ...), custom_call_target="tpu_custom_call" | custom-call | tf_op jit(solution)/shard_map/fourth/pallas_call | solution.py:466
Async XLA Ops:
  17.7 1.3 %collective-permute-start = (f32[256,128]{1,0:T(8,128)S(1)}, f32[256,128]{1,0:T(8,128)S(1)}, u32[]{:S(2)}, u32[]{:S(2)}) collective-permute-start(f32[256,128]{1,0:T(8,128)S(1)} %bitcast.10), channel_id=1, source_target_pairs={{0,1},{1,0},{2,3},{3,2},{4,5},{5,4},{6,7},{7,6},{8,9},{9,8},{10,11... | collective-permute-start | bytes 393224 | tf_op jit(solution)/shard_map/ppermute | solution.py:509
